TPU v7x, 32 devices: a 4x4x1 block of a 4x4x8 slice. The times are simulated.
32 devices in a mesh: prompts: 1 (over z), model: 4 (over y), resp: 8 (over x, core).
Axes of the slice: x: 4, y: 4, z: 1, core: 2. Of those that a mesh axis runs over, the one named last changes fastest.
The devices are a block of a 4x4x8 slice.
Arguments:
- x_prompt: bfloat16 [2048, 2048], P(('prompts', 'resp'))
- x_resp: bfloat16 [8, 1024, 2048], P(('prompts', 'resp'))
- targets: int32 [8, 1024], P(('prompts', 'resp'))
- resp_lens: int32 [8], P(('prompts', 'resp'))
- attn_gain: float32 [2, 2048], replicated
- w_query: bfloat16 [2, 2048, 16, 128], P(None, None, 'model')
- w_key: bfloat16 [2, 2048, 16, 128], P(None, None, 'model')
- w_value: bfloat16 [2, 2048, 16, 128], P(None, None, 'model')
- w_out: bfloat16 [2, 16, 128, 2048], P(None, 'model')
- mlp_gain: float32 [2, 2048], replicated
- w_gate: bfloat16 [2, 2048, 5504], P(None, None, 'model')
- w_up: bfloat16 [2, 2048, 5504], P(None, None, 'model')
- w_down: bfloat16 [2, 5504, 2048], P(None, 'model')
- final_gain: float32 [2048], replicated
- w_vocab: bfloat16 [2048, 32768], P(None, 'model')
Outputs:
- output: float32 [8, 1024], P(('prompts', 'resp'))
All inputs are finite; a program needn't handle non-finite values.
Results may differ from a plain program's by a relative error of at most 0.00244122.
Values are sent between devices in bfloat16 or wider.
A program may use at most 768 MiB of HBM per device.

v0:
```python
import jax
import jax.numpy as jnp
from jax import lax
from jax.sharding import PartitionSpec as P

EPS = 1e-6
ROPE_BASE = 10000.0


def rms_norm(acts_in, gain_vec):
    acts_f = acts_in.astype(jnp.float32)
    inv_rms = lax.rsqrt(jnp.mean(acts_f * acts_f, axis=-1, keepdims=True) + EPS)
    return (acts_f * inv_rms * gain_vec).astype(jnp.bfloat16)


def rotary(projected, positions):
    half_dim = projected.shape[-1] // 2
    frequency = ROPE_BASE ** (-jnp.arange(half_dim, dtype=jnp.float32) / half_dim)
    angles = positions.astype(jnp.float32)[..., None] * frequency
    cos_part = jnp.cos(angles)[..., None, :]
    sin_part = jnp.sin(angles)[..., None, :]
    lower_half = projected[..., :half_dim]
    upper_half = projected[..., half_dim:]
    return jnp.concatenate([lower_half * cos_part - upper_half * sin_part, upper_half * cos_part + lower_half * sin_part], axis=-1)


def attend(queries, keys, values, query_pos, key_pos):
    heads, head_dim = queries.shape[-2], queries.shape[-1]
    kv_heads = keys.shape[-2]
    grouped = queries.reshape(queries.shape[:-2] + (kv_heads, heads // kv_heads, head_dim))
    scores = jnp.einsum('...tkrd,...skd->...krts', grouped, keys, preferred_element_type=jnp.float32) * (head_dim ** -0.5)
    visible = (key_pos[None, :] <= query_pos[..., :, None])[..., None, None, :, :]
    scores = jnp.where(visible, scores, -jnp.inf)
    row_max = jnp.max(scores, axis=-1, keepdims=True)
    exp_scores = jnp.exp(scores - row_max)
    row_sum = jnp.moveaxis(jnp.sum(exp_scores, axis=-1), -1, -3)
    mixed = jnp.einsum('...krts,...skd->...tkrd', exp_scores.astype(jnp.bfloat16), values, preferred_element_type=jnp.float32)
    return (mixed / row_sum[..., None]).reshape(queries.shape).astype(jnp.bfloat16)


def solution(mesh):
    groups = mesh.shape['resp']
    row_axes = ('prompts', 'resp')
    head_spec = P(None, None, 'model', None)
    in_specs = (P(row_axes, None), P(row_axes, None, None), P(row_axes, None), P(row_axes), P(None, None), head_spec, head_spec, head_spec, P(None, 'model', None, None), P(None, None), P(None, None, 'model'), P(None, None, 'model'), P(None, 'model', None), P(None), P(None, 'model'))

    def device_step(x_prompt, x_resp, targets, resp_lens, attn_gain, w_query, w_key, w_value, w_out, mlp_gain, w_gate, w_up, w_down, final_gain, w_vocab):
        prompt_rows = x_prompt.shape[0]
        resp_len = x_resp.shape[1]
        prompt_len = prompt_rows * groups
        num_layers = w_query.shape[0]
        resp_pos = prompt_len + jnp.arange(resp_len)
        tok_pos = jnp.concatenate([lax.axis_index('resp') * prompt_rows + jnp.arange(prompt_rows), resp_pos])
        key_pos = jnp.concatenate([jnp.arange(prompt_len), resp_pos])
        residual = jnp.concatenate([x_prompt, x_resp[0]], axis=0)
        for layer_idx in range(num_layers):
            hidden = rms_norm(residual, attn_gain[layer_idx])
            keys = rotary(jnp.einsum('td,dhe->the', hidden, w_key[layer_idx], preferred_element_type=jnp.float32), tok_pos).astype(jnp.bfloat16)
            values = jnp.einsum('td,dhe->the', hidden, w_value[layer_idx], preferred_element_type=jnp.float32).astype(jnp.bfloat16)
            prompt_keys = lax.all_gather(keys[:prompt_rows], 'resp', axis=0, tiled=True)
            prompt_values = lax.all_gather(values[:prompt_rows], 'resp', axis=0, tiled=True)
            all_keys = jnp.concatenate([prompt_keys, keys[prompt_rows:]], axis=0)
            all_values = jnp.concatenate([prompt_values, values[prompt_rows:]], axis=0)
            query_pos = tok_pos
            if layer_idx == num_layers - 1:
                residual = residual[prompt_rows:]
                hidden = hidden[prompt_rows:]
                query_pos = resp_pos
            queries = rotary(jnp.einsum('td,dhe->the', hidden, w_query[layer_idx], preferred_element_type=jnp.float32), query_pos).astype(jnp.bfloat16)
            mixed = attend(queries, all_keys, all_values, query_pos, key_pos)
            attn_part = jnp.einsum('the,hed->td', mixed, w_out[layer_idx], preferred_element_type=jnp.float32)
            residual = (residual.astype(jnp.float32) + lax.psum(attn_part, 'model')).astype(jnp.bfloat16)
            hidden = rms_norm(residual, mlp_gain[layer_idx])
            gate = jnp.dot(hidden, w_gate[layer_idx], preferred_element_type=jnp.float32)
            up_proj = jnp.dot(hidden, w_up[layer_idx], preferred_element_type=jnp.float32)
            inner = (jax.nn.silu(gate) * up_proj).astype(jnp.bfloat16)
            down_part = jnp.dot(inner, w_down[layer_idx], preferred_element_type=jnp.float32)
            residual = (residual.astype(jnp.float32) + lax.psum(down_part, 'model')).astype(jnp.bfloat16)
        logits = jnp.dot(rms_norm(residual, final_gain), w_vocab, preferred_element_type=jnp.float32)
        vocab_local = logits.shape[-1]
        vocab_ids = lax.axis_index('model') * vocab_local + jnp.arange(vocab_local)
        row_max = lax.pmax(jnp.max(logits, axis=-1), 'model')
        exp_total = lax.psum(jnp.sum(jnp.exp(logits - row_max[:, None]), axis=-1), 'model')
        picked = lax.psum(jnp.sum(jnp.where(vocab_ids[None, :] == targets[0][:, None], logits, 0.0), axis=-1), 'model')
        log_probs = picked - row_max - jnp.log(exp_total)
        log_probs = jnp.where(jnp.arange(resp_len) < resp_lens[0], log_probs, 0.0)
        return log_probs[None, :]

    return jax.shard_map(device_step, mesh=mesh, in_specs=in_specs, out_specs=P(row_axes, None), check_vma=False)
```

profile of v0, /device:TPU:97, one launch (start us, length us, event | category | flops | bytes accessed | tf_op | source)
XLA Modules:
  0.0 1157.9 jit_solution(16334911752362392178)
XLA Ops:
  6.6 3.7 fusion.16
  11.0 2.5 fusion.159
  13.4 2.7 copy.44
  16.1 4.1 fusion.160
  20.2 2.6 copy.43
  22.9 5.4 fusion.18
  28.3 4.4 fusion.166
  32.7 4.5 fusion.165
  39.2 4.3 subtract_convert_fusion.1
  44.7 4.0 fusion.158
  48.6 5.4 fusion.99
  55.0 4.0 broadcast_compare_fusion
  59.0 13.6 %all-gather.7.cloned.1.call-done = bf16[2048,4,128]{0,2,1:T(8,128)(2,1)} async-done(((bf16[256,4,128]{0,2,1:T(8,128)(2,1)}), bf16[2048,4,128]{0,2,1:T(8,128)(2,1)}) %all-gather.7.cloned.1.call-update) | async-done | bytes 2097168 | tf_op jit(solution)/shard_map/all_gather | solution.py:60
  72.6 26.5 %fusion.163 = (f32[4,1280]{1,0:T(4,128)S(1)}, f32[4,1,1280,3072]{2,3,0,1:T(8,128)}) fusion(bf16[1280,4,64]{0,2,1:T(8,128)(2,1)} %get-tuple-element.24, bf16[1280,4,64]{0,2,1:T(8,128)(2,1)} %get-tuple-element.23, bf16[1280,4,64]{0,2,1:T(8,128)(2,1)S(1)} %get-tuple-element.29, bf16[1280,4,64]{0,2,1:T(8,128)(2,1)} %copy-done.14, ...), kind=kOutput, calls=%fused_computation.179 | convolution fusion | flops 4090489856 | bytes 71585792 | tf_op jit(solution)/shard_map/...tkrd,...skd->...krts/dot_general | solution.py:31
  99.2 20.2 %fusion = f32[4,1280]{1,0:T(4,128)S(1)} fusion(f32[4,1,1280,3072]{2,3,0,1:T(8,128)} %get-tuple-element.42, f32[4,1280]{1,0:T(4,128)S(1)} %get-tuple-element.41), kind=kLoop, calls=%fused_computation.2 | loop fusion | flops 31452160 | bytes 62955520 | tf_op jit(solution)/shard_map/reduce_sum | solution.py:36
  119.4 25.5 %fusion.73 = f32[1280,4,1,128]{0,3,1,2:T(8,128)} fusion(f32[4,1,1280,3072]{2,3,0,1:T(8,128)} %get-tuple-element.42, f32[4,1280]{1,0:T(4,128)S(1)} %get-tuple-element.41, bf16[1024,4,128]{2,0,1:T(8,128)(2,1)S(1)} %slice-done, bf16[2048,4,128]{2,0,1:T(8,128)(2,1)} %all-gather.5.cloned.1.call-done), kind=kOutput, calls=%fused_computation.92 | convolution fusion | flops 4064280576 | bytes 68702208 | tf_op jit(solution)/shard_map/...krts,...skd->...tkrd/dot_general | solution.py:37
  144.8 9.1 convolution_bitcast_fusion
  155.3 188.0 %all-reduce.6.cloned.1.call-done = f32[1280,2048]{1,0:T(8,128)} async-done(((f32[1280,2048]{1,0:T(8,128)}), f32[1280,2048]{1,0:T(8,128)}) %all-reduce.6.cloned.1.call-update) | async-done | bytes 10485776 | tf_op jit(solution)/shard_map/psum | solution.py:72
  343.3 9.0 fusion.20
  352.3 13.0 %fusion.49 = f32[1280,1376]{0,1:T(8,128)} fusion(bf16[2,2048,1376]{1,2,0:T(8,128)(2,1)} %param.25, bf16[1280,2048]{1,0:T(8,128)(2,1)} %get-tuple-element.14, f32[2048]{0:T(1024)S(1)} %bitcast.167, f32[1280]{0:T(1024)S(1)} %add_rsqrt_fusion.1), kind=kOutput, calls=%fused_computation.71 | convolution fusion | flops 7224688640 | bytes 17937408 | tf_op jit(solution)/shard_map/dot_general | solution.py:74
  365.3 51.6 %fusion.32 = f32[1280,2048]{1,0:T(8,128)} fusion(f32[1280,1376]{0,1:T(8,128)} %fusion.49, bf16[2,1376,2048]{2,1,0:T(8,128)(2,1)} %param.27, bf16[2,2048,1376]{1,2,0:T(8,128)(2,1)} %param.26, bf16[1280,2048]{1,0:T(8,128)(2,1)} %get-tuple-element.14, f32[2048]{0:T(1024)S(1)} %bitcast.168, f32[1280]{0:T(1024)S(1)} %add_rsqrt_fusion.1), kind=kOutput, calls=%fused_computation.53 | convolution fusion | flops 14449459200 | bytes 34059264 | tf_op jit(solution)/shard_map/dot_general | solution.py:77
  417.0 1.4 copy-done.5
  418.4 2.6 copy.46
  421.1 184.7 %all-reduce.8.cloned.1.call-done = f32[1280,2048]{1,0:T(8,128)} async-done(((f32[1280,2048]{1,0:T(8,128)}), f32[1280,2048]{1,0:T(8,128)}) %all-reduce.8.cloned.1.call-update) | async-done | bytes 10485776 | tf_op jit(solution)/shard_map/psum | solution.py:78
  605.7 9.5 fusion.13
  615.2 3.9 fusion.15
  619.2 2.9 fusion.167
  624.4 2.7 copy.47
  627.1 1.7 multiply_cosine_fusion.1
  628.8 2.0 broadcast_compare_fusion.1
  630.8 6.0 fusion.102
  638.7 6.6 fusion.68
  645.4 2.9 subtract_convert_fusion.3
  648.8 21.4 %fusion.4 = (f32[4,1024]{1,0:T(4,128)S(1)}, f32[4,3072,1024]{2,1,0:T(8,128)}) fusion(pred[1024,3072]{0,1:T(8,128)(4,1)S(1)} %broadcast_compare_fusion.1, bf16[1024,4,64]{0,2,1:T(8,128)(2,1)} %get-tuple-element.28, bf16[1024,4,64]{0,2,1:T(8,128)(2,1)} %get-tuple-element.27, bf16[1280,4,64]{0,2,1:T(8,128)(2,1)} %copy-done.16, ...), kind=kOutput, calls=%fused_computation.8 | convolution fusion | flops 3275223040 | bytes 57950208 | tf_op jit(solution)/shard_map/...tkrd,...skd->...krts/dot_general | solution.py:31
  670.2 21.2 %fusion.2 = f32[4,1024]{1,0:T(4,128)S(1)} fusion(f32[4,3072,1024]{2,1,0:T(8,128)} %get-tuple-element.44, f32[4,1024]{1,0:T(4,128)S(1)} %get-tuple-element.43, pred[1024,3072]{0,1:T(8,128)(4,1)S(1)} %broadcast_compare_fusion.1), kind=kLoop, calls=%fused_computation.6 | loop fusion | flops 50327552 | bytes 53510144 | tf_op jit(solution)/shard_map/reduce_sum | solution.py:36
  691.4 27.7 %convolution_bitcast_fusion.1 = f32[1024,2048]{1,0:T(8,128)} fusion(bf16[2,4,128,2048]{3,2,1,0:T(8,128)(2,1)} %param.23, f32[4,3072,1024]{2,1,0:T(8,128)} %get-tuple-element.44, f32[4,1024]{1,0:T(4,128)S(1)} %get-tuple-element.43, pred[1024,3072]{0,1:T(8,128)(4,1)S(1)} %broadcast_compare_fusion.1, bf16[1024,4,128]{2,0,1:T(8,128)(2,1)} %slice.152, ...), kind=kOutput, calls=%fused_computation.85 | convolution fusion | flops 5426380800 | bytes 67141632 | tf_op jit(solution)/shard_map/the,hed->td/dot_general | solution.py:71
  719.3 155.3 %all-reduce.10.cloned.1.call-done = f32[1024,2048]{1,0:T(8,128)} async-done(((f32[1024,2048]{1,0:T(8,128)}), f32[1024,2048]{1,0:T(8,128)}) %all-reduce.10.cloned.1.call-update) | async-done | bytes 8388624 | tf_op jit(solution)/shard_map/psum | solution.py:72
  874.6 5.4 fusion.27
  880.0 1.9 copy-done
  881.9 10.0 fusion.44
  891.9 23.8 %fusion.40 = f32[1024,2048]{1,0:T(8,128)} fusion(bf16[2,1376,2048]{2,1,0:T(8,128)(2,1)} %param.27, f32[1024,1376]{0,1:T(8,128)} %fusion.44, bf16[2,2048,1376]{1,2,0:T(8,128)(2,1)} %param.26, bf16[1024,2048]{1,0:T(8,128)(2,1)} %copy-done, f32[2048]{0:T(1024)S(1)} %bitcast.166, f32[1024]{0:T(1024)S(1)} %add_rsqrt_fusion.4), kind=kOutput, calls=%fused_computation.63 | convolution fusion | flops 11559567360 | bytes 29503488 | tf_op jit(solution)/shard_map/dot_general | solution.py:77
  916.5 154.2 %all-reduce.12.cloned.1.call-done = f32[1024,2048]{1,0:T(8,128)} async-done(((f32[1024,2048]{1,0:T(8,128)}), f32[1024,2048]{1,0:T(8,128)}) %all-reduce.12.cloned.1.call-update) | async-done | bytes 8388624 | tf_op jit(solution)/shard_map/psum | solution.py:78
  1070.7 5.9 fusion.24
  1076.6 2.3 copy-done.3
  1078.9 42.1 %fusion.164 = (f32[1024]{0:T(1024)S(1)}, f32[1024,8192]{1,0:T(8,128)}) fusion(bf16[2048,8192]{1,0:T(8,128)(2,1)} %param.29, f32[2048]{0:T(1024)S(1)} %copy-done.29, f32[1024]{0:T(1024)S(1)} %add_rsqrt_fusion.3, f32[1024,2048]{1,0:T(8,128)S(1)} %copy-done.3, bf16[1024,2048]{1,0:T(8,128)(2,1)S(1)} %copy-done.1), kind=kOutput, calls=%fused_computation.180 | convolution fusion | flops 34382807040 | bytes 79708160 | tf_op jit(solution)/shard_map/dot_general | solution.py:79
  1121.0 6.7 pmax.7
  1127.7 15.3 %select_reduce_fusion = (f32[1024]{0:T(1024)S(1)}, f32[1024]{0:T(1024)S(1)}) fusion(f32[1024,8192]{1,0:T(8,128)} %get-tuple-element.46, s32[8192]{0:T(1024)S(1)} %iota_add_fusion, s32[1024]{0:T(1024)S(1)} %bitcast.169, f32[1024]{0:T(1024)S(1)} %pmax.7), kind=kLoop, calls=%fused_computation.10 | loop fusion | flops 41940992 | bytes 33603584 | tf_op jit(solution)/shard_map/reduce_sum | solution.py:84
  1143.1 6.9 all-reduce
  (101 shorter events, 11.6 us)
Async XLA Ops:
  6.5 3.8 copy-start.23
  6.5 66.1 %all-gather.7.cloned.1.call-start = ((), (), s32[]{:S(2)}) async-start(), calls=%async_computation.1 | async-start | bytes 2359296 | tf_op jit(solution)/shard_map/all_gather | solution.py:60
  6.6 4.4 copy-start.9
  6.6 48.4 %copy-start.20 = (s32[1024]{0:T(1024)}, s32[1024]{0:T(1024)S(1)}, u32[]{:S(2)}) copy-start(s32[1024]{0:T(1024)S(1)} %iota_add_fusion.1) | copy-start | bytes 12292
  6.6 30.7 %copy-start.27 = (f32[64]{0:T(128)}, f32[64]{0:T(128)S(1)}, u32[]{:S(2)}) copy-start(f32[64]{0:T(128)S(1)} %multiply_power_fusion) | copy-start | bytes 772
  16.1 6.8 copy-start.2
  22.9 5.4 copy-start.18
  28.3 4.4 copy-start.6
  28.3 4.4 copy-start.19
  38.5 0.7 copy-start.10
  38.5 5.0 copy-start.12
  43.5 5.1 copy-start.14
  44.3 75.0 %all-gather.5.cloned.1.call-start = ((), (), s32[]{:S(2)}) async-start(), calls=%async_computation | async-start | bytes 2359296 | tf_op jit(solution)/shard_map/all_gather | solution.py:61
  54.0 45.1 %copy-start.8 = (bf16[1280,4,128]{2,0,1:T(8,128)(2,1)}, bf16[1280,4,128]{2,0,1:T(8,128)(2,1)S(1)}, u32[]{:S(2)}) copy-start(bf16[1280,4,128]{2,0,1:T(8,128)(2,1)S(1)} %fusion.99) | copy-start | bytes 3932164
  54.9 288.4 %all-reduce.6.cloned.1.call-start = ((), (), s32[]{:S(2)}) async-start(), calls=%async_computation.2 | async-start | bytes 20971520 | tf_op jit(solution)/shard_map/psum | solution.py:72
  99.1 20.2 %slice-start = ((bf16[1280,4,128]{2,0,1:T(8,128)(2,1)}), bf16[1024,4,128]{2,0,1:T(8,128)(2,1)S(1)}, s32[]{:S(2)}) async-start(bf16[1280,4,128]{2,0,1:T(8,128)(2,1)} %copy-done.8), calls=%async_computation.8 | async-start | bytes 2097152 | tf_op jit(solution)/shard_map/slice | solution.py:63
  154.0 0.7 copy-start.24
  154.0 451.7 %all-reduce.8.cloned.1.call-start = ((), (), s32[]{:S(2)}) async-start(), calls=%async_computation.3 | async-start | bytes 20971520 | tf_op jit(solution)/shard_map/psum | solution.py:78
  416.8 1.6 copy-start.5
  416.9 231.9 %all-gather.11.cloned.1.call-start = ((), (), s32[]{:S(2)}) async-start(), calls=%async_computation.5 | async-start | bytes 2359296 | tf_op jit(solution)/shard_map/all_gather | solution.py:60
  421.1 194.2 %copy-start.22 = (f32[1,2048]{1,0:T(1,128)S(1)}, f32[1,2048]{1,0:T(1,128)}, u32[]{:S(2)}) copy-start(f32[1,2048]{1,0:T(1,128)} %get-tuple-element.33) | copy-start | bytes 24580
  615.2 3.9 copy-start.17
  619.1 3.0 copy-start.7
  619.2 3.0 copy-start.11
  619.2 3.0 copy-start.13
  622.1 2.3 copy-start.4
  622.1 5.0 copy-start.28
  622.2 6.7 copy-start.21
  622.5 0.8 copy-start.15
  622.5 1.0 copy-start.16
  624.3 67.1 %all-gather.9.cloned.1.call-start = ((), (), s32[]{:S(2)}) async-start(), calls=%async_computation.4 | async-start | bytes 2359296 | tf_op jit(solution)/shard_map/all_gather | solution.py:61
  645.3 229.3 %all-reduce.10.cloned.1.call-start = ((), (), s32[]{:S(2)}) async-start(), calls=%async_computation.6 | async-start | bytes 16777216 | tf_op jit(solution)/shard_map/psum | solution.py:72
  719.2 162.7 %copy-start.25 = (f32[1,2048]{1,0:T(1,128)S(1)}, f32[1,2048]{1,0:T(1,128)}, u32[]{:S(2)}) copy-start(f32[1,2048]{1,0:T(1,128)} %get-tuple-element.31) | copy-start | bytes 24580
  719.2 351.4 %all-reduce.12.cloned.1.call-start = ((), (), s32[]{:S(2)}) async-start(), calls=%async_computation.7 | async-start | bytes 16777216 | tf_op jit(solution)/shard_map/psum | solution.py:78
  879.9 1.9 copy-start
  916.5 160.1 %copy-start.29 = (f32[2048]{0:T(1024)S(1)}, f32[2048]{0:T(1024)}, u32[]{:S(2)}) copy-start(f32[2048]{0:T(1024)} %param.28) | copy-start | bytes 24580
  1070.7 5.9 copy-start.1
  1070.7 8.2 copy-start.3
  1078.9 48.8 %copy-start.26 = (s32[1,1024]{1,0:T(1,128)S(1)}, s32[1,1024]{1,0:T(1,128)}, u32[]{:S(2)}) copy-start(s32[1,1024]{1,0:T(1,128)} %param.17) | copy-start | bytes 12292
Sparse Core Ops, SparseCore 0:
  44.5 28.1 all-gather.6
  74.2 23.4 all-gather.4
  154.1 189.0 all-reduce.5
  417.0 188.6 all-reduce.7
  624.5 24.3 all-gather.10
  650.3 23.4 all-gather.8
  719.3 155.1 all-reduce.9
  915.9 154.7 all-reduce.11
where the time goes:
time: 1170 us; the launch traced here: 1160 us
  waiting for transfers between devices  697 us (60%)
  matrix products  281 us (24%)
  other arithmetic  118 us (10%)
  local copies, waits for them, and re-layouts  33 us (3%)
  between operations  15.1 us (1%)
  blocking collectives  13.6 us (1%)
    psum x2, waiting for transfers between devices, device_step(): lax.psum(attn_part, 'model')  343 us
    psum x2, waiting for transfers between devices, device_step(): lax.psum(down_part, 'model')  339 us
    dot_general x2, matrix products, device_step(): jnp.dot(inner, w_down[layer_idx], preferred_element_type=jnp.float32)  75.4 us
    dot_general x2, matrix products, attend(): jnp.einsum('...tkrd,...skd->...krts', grouped, keys, preferred_element_ty...  47.8 us
    dot_general x1, matrix products, device_step(): jnp.dot(rms_norm(residual, final_gain), w_vocab, preferred_element_type=j...  42.1 us
    reduce_sum x2, other arithmetic, attend(): row_sum = jnp.moveaxis(jnp.sum(exp_scores, axis=-1), -1, -3)  41.4 us
    dot_general x2, matrix products, device_step(): jnp.einsum('the,hed->td', mixed, w_out[layer_idx], preferred_element_type...  36.9 us
    reduce_sum x5, other arithmetic, rms_norm(): inv_rms = lax.rsqrt(jnp.mean(acts_f * acts_f, axis=-1, keepdims=True) + EPS)  33.5 us
  transfers between devices with their start and end apart: 8, of which 6 were waited for; matrix products, arithmetic and copies ran while one was open for 11% of the time, Pallas kernels for 0%

commit v1 on v0

v1 whole, which is shorter than its diff:
```python
import functools

import jax
import jax.numpy as jnp
from jax import lax
from jax.experimental import pallas as pl
from jax.experimental.pallas import tpu as pltpu
from jax.sharding import PartitionSpec as P

EPS = 1e-6
ROPE_BASE = 10000.0
LOG2E = 1.4426950408889634
VMEM_BYTES = 67043328
ROWS = 64
BF = jnp.bfloat16
F32 = jnp.float32
ANY = pl.BlockSpec(memory_space=pl.ANY)
VM = pl.BlockSpec(memory_space=pltpu.VMEM)


def remote(src, dst, send, recv, axis, where):
    return pltpu.make_async_remote_copy(src_ref=src, dst_ref=dst, send_sem=send, recv_sem=recv, device_id={axis: where}, device_id_type=pl.DeviceIdType.MESH)


def entry_barrier(peers):
    barrier = pltpu.get_barrier_semaphore()
    for axis, where in peers:
        pl.semaphore_signal(barrier, inc=1, device_id={axis: where}, device_id_type=pl.DeviceIdType.MESH)
    pl.semaphore_wait(barrier, len(peers))


def ds(start, size):
    return pl.ds(pl.multiple_of(start, size), size)


def dot(a, b):
    return jnp.dot(a, b, preferred_element_type=F32)


class Gather:
    def __init__(self, buf, send, recv, me):
        self.buf, self.send, self.recv, self.me = buf, send, recv, me
        self.right, self.left = lax.rem(me + 1, 4), lax.rem(me + 3, 4)
        self.opp = lax.rem(me + 2, 4)
        self.half = buf.shape[2] // 2

    def _copy(self, kind, c, block):
        ref = self.buf.at[c, block]
        if kind == 2:
            ref = ref.at[pl.ds(0, self.half)]
        if kind == 3:
            ref = ref.at[pl.ds(self.half, self.half)]
        return remote(ref, ref, self.send.at[kind, c], self.recv.at[kind, c], 'model', self.right if kind in (0, 2) else self.left)

    def start(self, c):
        self._copy(0, c, self.me).start()
        self._copy(1, c, self.me).start()

    def forward(self, c):
        self._copy(0, c, self.left).wait_recv()
        self._copy(2, c, self.left).start()
        self._copy(1, c, self.right).wait_recv()
        self._copy(3, c, self.right).start()

    def finish(self, c):
        self._copy(2, c, self.opp).wait_recv()
        self._copy(3, c, self.opp).wait_recv()

    def drain(self, c):
        self._copy(0, c, self.me).wait_send()
        self._copy(1, c, self.me).wait_send()
        self._copy(2, c, self.left).wait_send()
        self._copy(3, c, self.right).wait_send()


def norm_rows(src, dst, gain_ref, rows, width, tile=256):
    def square(n, total):
        block = src(ds(n * tile, tile)).astype(F32)
        sq = block * block
        for i in range(tile // 128):
            total = total + sq[:, i * 128:(i + 1) * 128]
        return total

    total = lax.fori_loop(0, width // tile, square, jnp.zeros((rows, 128), F32))
    inv = lax.rsqrt(jnp.sum(total, axis=-1, keepdims=True) * (1.0 / width) + EPS)

    def scale(n, carry):
        cols = ds(n * tile, tile)
        dst(cols, (src(cols).astype(F32) * inv * gain_ref[:, cols]).astype(BF))
        return carry

    lax.fori_loop(0, width // tile, scale, 0)


def attention_kernel(first, chunks, width, scale, *refs):
    if first:
        (xp, xr, gain, wq, wk, wv, cos, sin, o_out, x_v, h_v, q_v, k_v, v_v, kp_v, vp_v, acc_v, m_v, l_v, o_v, load, gs, gr, ks, kr, os_, or_) = refs
    else:
        (hin, wq, wk, wv, cos, sin, o_out, h_v, q_v, k_v, v_v, kp_v, vp_v, acc_v, m_v, l_v, o_v, load, gs, gr, ks, kr, os_, or_) = refs
    me = lax.axis_index('model')
    r = lax.axis_index('resp')
    chip = r // 2
    partner = r + 1 - 2 * lax.rem(r, 2)
    xs = [lax.rem(r + 2, 8), lax.rem(r + 6, 8), lax.rem(r + 4, 8)]
    gather = None if first else Gather(h_v, gs, gr, me)
    q_rows = chunks * 256 if first else (chunks - 1) * 256
    head_dim = 128
    heads = width // head_dim
    log_scale = scale * LOG2E

    loads = []
    if first:
        loads.append(pltpu.make_async_copy(xp, x_v.at[0], load.at[0]))
        for c in range(1, chunks):
            loads.append(pltpu.make_async_copy(xr.at[0, pl.ds((c - 1) * 256, 256)], x_v.at[c], load.at[c]))
    else:
        for c in range(chunks):
            loads.append(pltpu.make_async_copy(hin.at[c], h_v.at[c, me], load.at[c]))
    for cp in loads:
        cp.start()
    entry_barrier([('model', lax.rem(me + k, 4)) for k in (1, 2, 3)] + [('resp', partner)] + [('resp', x) for x in xs])

    def project(c, with_q):
        base = c * 256
        cs, sn = cos[pl.ds(base, 256), :], sin[pl.ds(base, 256), :]

        def rope(y):
            return y * cs + pltpu.roll(y, 64, 1) * sn

        h = h_v.at[c]
        for which, w in enumerate((wk, wv, wq)):
            if which == 2 and not with_q:
                continue
            for n in range(width // 256):
                y = dot(h[...].reshape(256, h.shape[-1]), w[:, pl.ds(n * 256, 256)])
                for i in range(2):
                    part = y[:, i * 128:(i + 1) * 128]
                    if which != 1:
                        part = rope(part)
                    part = part.astype(BF)
                    cols = pl.ds(n * 256 + i * 128, 128)
                    if which == 2:
                        q_v[pl.ds(base - (0 if first else 256), 256), cols] = part
                    elif c == 0:
                        (kp_v, vp_v)[which][r, :, cols] = part
                    else:
                        (k_v, v_v)[which][pl.ds(base - 256, 256), cols] = part

    def kv_copy(which, kind, block):
        ref = (kp_v, vp_v)[which].at[block]
        where = xs[kind] if kind < 3 else partner
        return remote(ref, ref, ks.at[which, kind], kr.at[which, kind], 'resp', where)

    origin = [xs[1], xs[0], xs[2]]
    other = [lax.rem(o + 8 + 1 - 2 * lax.rem(o, 2), 8) for o in origin]

    def kv_start():
        for which in range(2):
            for kind in (3, 0, 1, 2):
                kv_copy(which, kind, r).start()

    def kv_pass(kind):
        for which in range(2):
            kv_copy(which, kind, origin[kind]).wait_recv()
            kv_copy(which, 4 + kind, origin[kind]).start()

    def kv_wait(kind, block):
        for which in range(2):
            kv_copy(which, kind, block).wait_recv()

    if first:
        for c in range(chunks):
            loads[c].wait()
            norm_rows(lambda cols, c=c: x_v[c, :, cols], lambda cols, val, c=c: h_v.__setitem__((c, slice(None), cols), val), gain, 256, x_v.shape[-1])
            project(c, True)
            if c == 0:
                kv_start()
    else:
        loads[0].wait()
        gather.start(0)
        loads[1].wait()
        gather.start(1)
        for c in range(chunks + 1):
            if c < chunks:
                gather.forward(c)
                if c + 2 < chunks:
                    loads[c + 2].wait()
                    gather.start(c + 2)
            if c > 0:
                gather.finish(c - 1)
                project(c - 1, c > 1)
                if c == 1:
                    kv_start()

    rows_i = lax.broadcasted_iota(jnp.int32, (256, 256), 0)
    cols_i = lax.broadcasted_iota(jnp.int32, (256, 256), 1)
    causal = cols_i <= rows_i

    def step(q, k, v, m, l, acc, mask=False):
        s = lax.dot_general(q, k, (((1,), (1,)), ((), ())), preferred_element_type=F32)
        if mask:
            s = jnp.where(causal, s, -jnp.inf)
        m_new = jnp.maximum(m, jnp.max(s, axis=-1, keepdims=True))
        p = jnp.exp2((s - m_new) * log_scale)
        alpha = jnp.exp2((m - m_new) * log_scale)
        l = l * alpha + jnp.sum(p, axis=-1, keepdims=True)
        acc = acc * alpha + dot(p.astype(BF), v)
        return m_new, l, acc

    def load_state(row, n):
        return m_v[n, pl.ds(row, 256), 0:1], l_v[n, pl.ds(row, 256), 0:1], acc_v[pl.ds(row, 256), pl.ds(n * 128, 128)]

    def save_state(row, n, state):
        m, l, acc = state
        m_v[n, pl.ds(row, 256), :] = jnp.broadcast_to(m, (256, 128))
        l_v[n, pl.ds(row, 256), :] = jnp.broadcast_to(l, (256, 128))
        acc_v[pl.ds(row, 256), pl.ds(n * 128, 128)] = acc

    def fresh():
        return jnp.full((256, 1), -jnp.inf, F32), jnp.zeros((256, 1), F32), jnp.zeros((256, 128), F32)

    def chip_keys(x, n):
        cols = pl.ds(n * 128, 128)
        return (kp_v[pl.ds(2 * x, 2), :, cols].reshape(512, 128), vp_v[pl.ds(2 * x, 2), :, cols].reshape(512, 128))

    base_q = 256 if first else 0
    def own(j, carry):
        row = pl.multiple_of(j * 256, 256)
        for n in range(heads):
            cols = pl.ds(n * 128, 128)
            q = q_v[pl.ds(base_q + row, 256), cols]
            state = step(q, k_v[pl.ds(row, 256), cols], v_v[pl.ds(row, 256), cols], *fresh(), mask=True)

            def before(b, state, q=q, cols=cols):
                keys = ds(b * 256, 256)
                return step(q, k_v[keys, cols], v_v[keys, cols], *state)

            state = lax.fori_loop(0, j, before, state)
            save_state(base_q + row, n, state)
        return carry

    lax.fori_loop(0, chunks - 1, own, 0)

    if first:
        for n in range(heads):
            cols = pl.ds(n * 128, 128)
            save_state(0, n, step(q_v[pl.ds(0, 256), cols], kp_v[r, :, cols], vp_v[r, :, cols], *fresh(), mask=True))

    kv_pass(0)
    kv_pass(1)
    kv_wait(3, partner)
    kv_pass(2)
    if first:
        @pl.when(partner < r)
        def _():
            for n in range(heads):
                cols = pl.ds(n * 128, 128)
                save_state(0, n, step(q_v[pl.ds(0, 256), cols], kp_v[partner, :, cols], vp_v[partner, :, cols], *load_state(0, n)))

    for kind in range(3):
        kv_wait(4 + kind, other[kind])

    def o_copy(c, k):
        owner = lax.rem(me + k, 4)
        dst = o_out.at[c, :, ds(me * width, width)]
        return remote(o_v.at[c, owner], dst, os_.at[k - 1, c], or_.at[k - 1, c], 'model', owner)

    def own_copy(c):
        return pltpu.make_async_copy(o_v.at[c, me], o_out.at[c, :, ds(me * width, width)], load.at[c])

    def emit(c, n, state):
        m, l, acc = state
        out = (acc / l).astype(BF)
        for b in range(4):
            o_v[c, b, :, pl.ds(n * 128, 128)] = out[b * ROWS:(b + 1) * ROWS]

    def send(c):
        for k in (2, 1, 3):
            o_copy(c, k).start()
        own_copy(c).start()

    if first:
        for n in range(heads):
            def earlier(x, state, n=n):
                k, v = chip_keys(x, n)
                return step(q_v[pl.ds(0, 256), pl.ds(n * 128, 128)], k, v, *state)
            emit(0, n, lax.fori_loop(0, chip, earlier, load_state(0, n)))
        send(0)

    out_chunks = chunks if first else chunks - 1
    for c in range(1 if first else 0, out_chunks):
        row = c * 256
        for n in range(heads):
            q = q_v[pl.ds(row, 256), pl.ds(n * 128, 128)]

            def prompt(x, state, q=q, n=n):
                k, v = chip_keys(x, n)
                return step(q, k, v, *state)
            emit(c, n, lax.fori_loop(0, 4, prompt, load_state(row, n)))
        send(c)

    for c in range(out_chunks):
        for k in (1, 2, 3):
            o_copy(c, k).wait_recv()
            o_copy(c, k).wait_send()
        own_copy(c).wait()
    for which in range(2):
        for kind in range(7):
            kv_copy(which, kind, r if kind < 4 else origin[kind - 4]).wait_send()
    if not first:
        for c in range(chunks):
            gather.drain(c)


def attention(first, collective, hidden, gain, wq, wk, wv, cos, sin):
    width = wq.shape[-1]
    model_dim = wq.shape[0]
    chunks = 5
    outs = chunks if first else chunks - 1
    scale = 128 ** -0.5
    scratch = []
    if first:
        scratch.append(pltpu.VMEM((chunks, 256, model_dim), BF))
        scratch.append(pltpu.VMEM((chunks, 256, model_dim), BF))
    else:
        scratch.append(pltpu.VMEM((chunks, 4, ROWS, model_dim), BF))
    scratch += [
        pltpu.VMEM((outs * 256, width), BF),
        pltpu.VMEM((1024, width), BF),
        pltpu.VMEM((1024, width), BF),
        pltpu.VMEM((8, 256, width), BF),
        pltpu.VMEM((8, 256, width), BF),
        pltpu.VMEM((outs * 256, width), F32),
        pltpu.VMEM((width // 128, outs * 256, 128), F32),
        pltpu.VMEM((width // 128, outs * 256, 128), F32),
        pltpu.VMEM((outs, 4, ROWS, width), BF),
        pltpu.SemaphoreType.DMA((chunks,)),
        pltpu.SemaphoreType.DMA((4, chunks)),
        pltpu.SemaphoreType.DMA((4, chunks)),
        pltpu.SemaphoreType.DMA((2, 7)),
        pltpu.SemaphoreType.DMA((2, 7)),
        pltpu.SemaphoreType.DMA((3, outs)),
        pltpu.SemaphoreType.DMA((3, outs)),
    ]
    args = (*hidden, gain, wq, wk, wv, cos, sin) if first else (*hidden, wq, wk, wv, cos, sin)
    specs = [ANY] * len(hidden) + [VM] * (len(args) - len(hidden))
    return pl.pallas_call(
        functools.partial(attention_kernel, first, chunks, width, scale),
        name=f'attention{collective}',
        out_shape=jax.ShapeDtypeStruct((outs, ROWS, 4 * width), BF),
        in_specs=specs,
        out_specs=ANY,
        scratch_shapes=scratch,
        compiler_params=pltpu.CompilerParams(collective_id=collective, has_side_effects=True, vmem_limit_bytes=VMEM_BYTES),
        cost_estimate=pl.CostEstimate(flops=30_000_000_000, bytes_accessed=20_000_000, transcendentals=0),
    )(*args)


def mlp_kernel(first, layer, chunks, *refs):
    if first:
        (o_in, xp, xr, gain, next_gain, wo, wg, wu, wd, x_out, h_out, wo_v, wg_v, wu_v, wd_v, o_v, x_v, u_v, si_v, ri_v, load, wl, gs, gr, is_, ir) = refs
    else:
        (o_in, x_in, gain, next_gain, wo, wg, wu, wd, h_out, wo_v, wg_v, wu_v, wd_v, o_v, x_v, u_v, si_v, ri_v, load, wl, gs, gr, is_, ir) = refs
    me = lax.axis_index('model')
    dim = x_v.shape[-1]
    ffn = wg_v.shape[-1]
    rows = chunks * ROWS
    gather = Gather(u_v, gs, gr, me)
    start = [pltpu.make_async_copy(o_in, o_v, load.at[0])]
    start += [pltpu.make_async_copy(wo, wo_v, wl.at[0])]
    if first:
        start += [pltpu.make_async_copy(xp.at[ds(me * ROWS, ROWS)], x_v.at[0], load.at[1])]
        start += [pltpu.make_async_copy(xr.at[0, ds((c - 1) * 256 + me * ROWS, ROWS)], x_v.at[c], load.at[1 + c]) for c in range(1, chunks)]
    else:
        start += [pltpu.make_async_copy(x_in.at[pl.ds(1, chunks)], x_v, load.at[1])]
    weights = [pltpu.make_async_copy(wg.at[layer], wg_v, wl.at[1]), pltpu.make_async_copy(wu.at[layer], wu_v, wl.at[2])]
    downs = [pltpu.make_async_copy(wd.at[lax.rem(me + k, 4)], wd_v.at[k], wl.at[3 + k]) for k in range(4)]
    for cp in start + weights + downs:
        cp.start()
    entry_barrier([('model', lax.rem(me + k, 4)) for k in (1, 2, 3)])
    for cp in start:
        cp.wait()

    def outproj(n, carry):
        cols = ds(n * 256, 256)
        y = dot(o_v[...].reshape(rows, dim), wo_v[:, cols])
        x_v[:, :, cols] = (x_v[:, :, cols].reshape(rows, 256).astype(F32) + y).astype(BF).reshape(chunks, ROWS, 256)
        return carry

    lax.fori_loop(0, dim // 256, outproj, 0)

    for c in range(chunks):
        norm_rows(lambda cols, c=c: x_v[c, :, cols], lambda cols, val, c=c: u_v.__setitem__((c, me, slice(None), cols), val), gain, ROWS, dim)
        if c < 2:
            gather.start(c)
    for cp in weights:
        cp.wait()

    def i_send(c, k):
        return remote(si_v.at[c, lax.rem(me + k, 4)], ri_v.at[3 - k, c], is_.at[k - 1, c], ir.at[k - 1, c], 'model', lax.rem(me + k, 4))

    def i_recv(c, q):
        ref = ri_v.at[q - 1, c]
        return remote(ref, ref, is_.at[3 - q, c], ir.at[3 - q, c], 'model', lax.rem(me + q, 4))

    full = ffn // 256

    def gate_up(c):
        def tile(cols, size):
            lhs = u_v[c].reshape(4 * ROWS, dim)
            g = dot(lhs, wg_v[:, cols])
            p = dot(lhs, wu_v[:, cols])
            si_v[c, :, :, cols] = (g * jax.nn.sigmoid(g) * p).astype(BF).reshape(4, ROWS, size)

        def body(n, carry):
            tile(ds(n * 256, 256), 256)
            return carry

        lax.fori_loop(0, full, body, 0)
        if ffn % 256:
            tile(pl.ds(full * 256, ffn % 256), ffn % 256)

    def down(lo, hi):
        size = hi - lo

        def body(n, carry):
            cols = ds(n * 256, 256)
            y = dot(si_v[lo:hi, me].reshape(size * ROWS, ffn), wd_v[0, :, cols])
            for q in (1, 2, 3):
                y = y + dot(ri_v[q - 1, lo:hi].reshape(size * ROWS, ffn), wd_v[q, :, cols])
            x_v[lo:hi, :, cols] = (x_v[lo:hi, :, cols].reshape(size * ROWS, 256).astype(F32) + y).astype(BF).reshape(size, ROWS, 256)
            return carry

        lax.fori_loop(0, dim // 256, body, 0)
        for c in range(lo, hi):
            norm_rows(lambda cols, c=c: x_v[c, :, cols], lambda cols, val, c=c: o_v.__setitem__((c, slice(None), cols), val), next_gain, ROWS, dim)

    for c in range(chunks + 1):
        if c < chunks:
            gather.forward(c)
            if c + 2 < chunks:
                gather.start(c + 2)
        if c > 0:
            gather.finish(c - 1)
            gate_up(c - 1)
            for k in (2, 1, 3):
                i_send(c - 1, k).start()
    for cp in downs:
        cp.wait()
    split = (chunks + 1) // 2
    outs = []
    for part, (lo, hi) in enumerate(((0, split), (split, chunks))):
        for c in range(lo, hi):
            for q in (1, 2, 3):
                i_recv(c, q).wait_recv()
        down(lo, hi)
        outs.append(pltpu.make_async_copy(o_v.at[pl.ds(lo, hi - lo)], h_out.at[pl.ds(lo, hi - lo)], load.at[part]))
        if first:
            outs.append(pltpu.make_async_copy(x_v.at[pl.ds(lo, hi - lo)], x_out.at[pl.ds(lo, hi - lo)], load.at[2 + part]))
        for cp in outs[-2 if first else -1:]:
            cp.start()
    for cp in outs:
        cp.wait()
    for c in range(chunks):
        gather.drain(c)
        for k in (1, 2, 3):
            i_send(c, k).wait_send()


def mlp(first, layer, collective, o_in, rows_in, gain, next_gain, wo, wg, wu, wd):
    chunks, _, dim = o_in.shape
    ffn = wg.shape[-1]
    args = (o_in, *rows_in, gain, next_gain, wo, wg, wu, wd)
    specs = [ANY] * (1 + len(rows_in)) + [VM, VM] + [ANY] * 4
    out = jax.ShapeDtypeStruct((chunks, ROWS, dim), BF)
    return pl.pallas_call(
        functools.partial(mlp_kernel, first, layer, chunks),
        name=f'mlp{collective}',
        out_shape=(out, out) if first else out,
        in_specs=specs,
        out_specs=(ANY, ANY) if first else ANY,
        scratch_shapes=[
            pltpu.VMEM((dim, dim), BF),
            pltpu.VMEM((dim, ffn), BF),
            pltpu.VMEM((dim, ffn), BF),
            pltpu.VMEM((4, ffn, dim), BF),
            pltpu.VMEM((chunks, ROWS, dim), BF),
            pltpu.VMEM((chunks, ROWS, dim), BF),
            pltpu.VMEM((chunks, 4, ROWS, dim), BF),
            pltpu.VMEM((chunks, 4, ROWS, ffn), BF),
            pltpu.VMEM((3, chunks, ROWS, ffn), BF),
            pltpu.SemaphoreType.DMA((6,)),
            pltpu.SemaphoreType.DMA((7,)),
            pltpu.SemaphoreType.DMA((4, chunks)),
            pltpu.SemaphoreType.DMA((4, chunks)),
            pltpu.SemaphoreType.DMA((3, chunks)),
            pltpu.SemaphoreType.DMA((3, chunks)),
        ],
        compiler_params=pltpu.CompilerParams(collective_id=collective, has_side_effects=True, vmem_limit_bytes=VMEM_BYTES),
        cost_estimate=pl.CostEstimate(flops=80_000_000_000, bytes_accessed=50_000_000, transcendentals=0),
    )(*args)


def head_kernel(chunks, tiles, h_in, wv, target, lens, out, wv_v, u_v, m_v, l_v, p_v, st_v, load, wl, gs, gr, ss, sr):
    me = lax.axis_index('model')
    dim = u_v.shape[-1]
    vocab = wv_v.shape[-1]
    gather = Gather(u_v, gs, gr, me)
    rows = [pltpu.make_async_copy(h_in.at[c], u_v.at[c, me], load.at[c]) for c in range(chunks)]
    span = vocab // tiles
    weights = [pltpu.make_async_copy(wv.at[:, pl.ds(n * span, span)], wv_v.at[:, pl.ds(n * span, span)], wl.at[n]) for n in range(tiles)]
    for cp in rows + weights:
        cp.start()
    entry_barrier([('model', lax.rem(me + k, 4)) for k in (1, 2, 3)])
    for c in range(2):
        rows[c].wait()
        gather.start(c)
    lane = lax.broadcasted_iota(jnp.int32, (256, 128), 1)

    def logits(c, n):
        cols = ds(n * 512, 512)
        s = dot(u_v[c].reshape(256, dim), wv_v[:, cols])
        parts = [s[:, i * 128:(i + 1) * 128] for i in range(4)]
        m = m_v[...]
        top = jnp.maximum(jnp.maximum(parts[0], parts[1]), jnp.maximum(parts[2], parts[3]))
        m_new = jnp.maximum(m, top)
        total = l_v[...] * jnp.exp2((m - m_new) * LOG2E)
        picked = p_v[...]
        wanted = target[pl.ds(c * 256, 256), :] - me * vocab - n * 512
        for i in range(4):
            total = total + jnp.exp2((parts[i] - m_new) * LOG2E)
            picked = picked + jnp.where(wanted - i * 128 == lane, parts[i], 0.0)
        m_v[...] = m_new
        l_v[...] = total
        p_v[...] = picked

    def vocab_pass(c):
        m_v[...] = jnp.full_like(m_v, -jnp.inf)
        l_v[...] = jnp.zeros_like(l_v)
        p_v[...] = jnp.zeros_like(p_v)
        per = span // 512
        if c == 0:
            for t in range(tiles):
                weights[t].wait()
                lax.fori_loop(t * per, (t + 1) * per, lambda n, carry: (logits(c, n), carry)[1], 0)
        else:
            lax.fori_loop(0, vocab // 512, lambda n, carry: (logits(c, n), carry)[1], 0)
        m = m_v[...]
        top = jnp.max(m, axis=-1, keepdims=True)
        total = jnp.sum(l_v[...] * jnp.exp2((m - top) * LOG2E), axis=-1, keepdims=True)
        picked = jnp.sum(p_v[...], axis=-1, keepdims=True)
        stat = jnp.where(lane == 0, top, jnp.where(lane == 1, total, picked))
        st_v[me, :, pl.ds(c * 256, 256)] = stat.T[:8]

    for c in range(chunks + 1):
        if c < chunks:
            gather.forward(c)
            if c + 2 < chunks:
                rows[c + 2].wait()
                gather.start(c + 2)
        if c > 0:
            gather.finish(c - 1)
            vocab_pass(c - 1)

    def st_copy(k, block):
        return remote(st_v.at[block], st_v.at[block], ss.at[k - 1], sr.at[k - 1], 'model', lax.rem(me + k, 4))

    for k in (2, 1, 3):
        st_copy(k, me).start()
    for k in (1, 2, 3):
        st_copy(k, lax.rem(me + 4 - k, 4)).wait_recv()
    tops = [st_v[s, 0:1, :] for s in range(4)]
    top = jnp.maximum(jnp.maximum(tops[0], tops[1]), jnp.maximum(tops[2], tops[3]))
    total = jnp.zeros_like(top)
    picked = jnp.zeros_like(top)
    for s in range(4):
        total = total + st_v[s, 1:2, :] * jnp.exp2((tops[s] - top) * LOG2E)
        picked = picked + st_v[s, 2:3, :]
    value = picked - top - jnp.log(total)
    token = lax.broadcasted_iota(jnp.int32, value.shape, 1)
    out[...] = jnp.where(token < lens[0], value, 0.0)
    for k in (1, 2, 3):
        st_copy(k, me).wait_send()
    for c in range(chunks):
        gather.drain(c)


def head(collective, h_in, wv, target, lens):
    chunks, _, dim = h_in.shape
    vocab = wv.shape[-1]
    tiles = 4
    return pl.pallas_call(
        functools.partial(head_kernel, chunks, tiles),
        name=f'head{collective}',
        out_shape=jax.ShapeDtypeStruct((1, chunks * 256), F32),
        in_specs=[ANY, ANY, VM, pl.BlockSpec(memory_space=pltpu.SMEM)],
        out_specs=VM,
        scratch_shapes=[
            pltpu.VMEM((dim, vocab), BF),
            pltpu.VMEM((chunks, 4, ROWS, dim), BF),
            pltpu.VMEM((256, 128), F32),
            pltpu.VMEM((256, 128), F32),
            pltpu.VMEM((256, 128), F32),
            pltpu.VMEM((4, 8, chunks * 256), F32),
            pltpu.SemaphoreType.DMA((chunks,)),
            pltpu.SemaphoreType.DMA((tiles,)),
            pltpu.SemaphoreType.DMA((4, chunks)),
            pltpu.SemaphoreType.DMA((4, chunks)),
            pltpu.SemaphoreType.DMA((3,)),
            pltpu.SemaphoreType.DMA((3,)),
        ],
        compiler_params=pltpu.CompilerParams(collective_id=collective, has_side_effects=True, vmem_limit_bytes=VMEM_BYTES),
        cost_estimate=pl.CostEstimate(flops=40_000_000_000, bytes_accessed=50_000_000, transcendentals=0),
    )(h_in, wv, target, lens)


def rope_tables(prompt_rows, resp_len, groups):
    half = 64
    freq = ROPE_BASE ** (-jnp.arange(half, dtype=F32) / half)
    pos = jnp.concatenate([lax.axis_index('resp') * prompt_rows + jnp.arange(prompt_rows), prompt_rows * groups + jnp.arange(resp_len)])
    angles = pos.astype(F32)[:, None] * freq
    c, s = jnp.cos(angles), jnp.sin(angles)
    return jnp.concatenate([c, c], axis=-1), jnp.concatenate([-s, s], axis=-1)


def whole(w):
    piece = w.shape[0] // 8
    part = lax.dynamic_slice_in_dim(w, lax.axis_index('resp') * piece, piece, 0)
    return lax.all_gather(part, ('model', 'resp'), axis=0, tiled=True)


def solution(mesh):
    groups = mesh.shape['resp']
    row_axes = ('prompts', 'resp')
    head_spec = P(None, None, 'model', None)
    in_specs = (P(row_axes, None), P(row_axes, None, None), P(row_axes, None), P(row_axes), P(None, None), head_spec, head_spec, head_spec, P(None, 'model', None, None), P(None, None), P(None, None, 'model'), P(None, None, 'model'), P(None, 'model', None), P(None), P(None, 'model'))

    def device_step(x_prompt, x_resp, targets, resp_lens, attn_gain, w_query, w_key, w_value, w_out, mlp_gain, w_gate, w_up, w_down, final_gain, w_vocab):
        dim = x_prompt.shape[-1]
        resp_len = x_resp.shape[1]
        width = w_query.shape[2] * w_query.shape[3]
        layers = w_query.shape[0]
        cos, sin = rope_tables(x_prompt.shape[0], resp_len, groups)
        flat = [[w[l].reshape(dim, width) for w in (w_query, w_key, w_value)] for l in range(layers)]
        outs = [whole(w_out[l].reshape(width, dim)) for l in range(layers)]
        downs = [whole(w_down[l]).reshape(4, w_down.shape[1], dim) for l in range(layers)]
        target = jnp.broadcast_to(targets[0][:, None], (resp_len, 128))
        o = attention(True, 0, (x_prompt, x_resp), attn_gain[0:1], *flat[0], cos, sin)
        x, h = mlp(True, 0, 1, o, (x_prompt, x_resp), mlp_gain[0:1], attn_gain[1:2], outs[0], w_gate, w_up, downs[0])
        o = attention(False, 2, (h,), None, *flat[1], cos, sin)
        h = mlp(False, 1, 3, o, (x,), mlp_gain[1:2], final_gain[None, :], outs[1], w_gate, w_up, downs[1])
        return head(4, h, w_vocab, target, resp_lens)

    return jax.shard_map(device_step, mesh=mesh, in_specs=in_specs, out_specs=P(row_axes, None), check_vma=False)
```

time: 1170 us -> 805 us (0.69)
  waiting for transfers between devices: 697 us -> 120 us
  Pallas kernels: 0 us -> 525 us
  matrix products: 281 us -> 0 us
  other arithmetic: 118 us -> 3.84 us
  local copies, waits for them, and re-layouts: 33 us -> 136 us
  blocking collectives: 13.6 us -> 0 us
    psum x4 -> x0, waiting for transfers between devices: 682 us -> none  [the longest x2 343 us: device_step(): lax.psum(attn_part, 'model')]
    pallas_call x0 -> x5, Pallas kernels: none -> 525 us  [the longest x2 230 us: attention(): pl.pallas_call(functools.partial(attention_kernel, first, chunks, width,...]
    dot_general x12 -> x0, matrix products: 262 us -> none  [the longest x2 75.4 us: device_step(): jnp.dot(inner, w_down[layer_idx], preferred_element_type=jnp.float32)]
    all_gather x4, waiting for transfers between devices: 14.2 us -> 120 us  [whole(): return lax.all_gather(part, ('model', 'resp'), axis=0, tiled=True)]
    reduce_sum x8 -> x0, other arithmetic: 90.2 us -> none  [the longest x2 41.4 us: attend(): row_sum = jnp.moveaxis(jnp.sum(exp_scores, axis=-1), -1, -3)]
    unnamed x64 -> x17, local copies, waits for them, and re-layouts: 18.7 us -> 104 us
    unnamed x4 -> x0, matrix products: 18.4 us -> none
  transfers between devices with their start and end apart: 8 -> 4, of which waited for: 6 -> 2; matrix products, arithmetic and copies ran while one was open for 11% -> 15% of each run, Pallas kernels for 0% -> 45%
where the time goes in v1:
time: 805 us; the launch traced here: 799 us
  Pallas kernels  525 us (65%)
  local copies, waits for them, and re-layouts  136 us (17%)
  waiting for transfers between devices  120 us (15%)
  between operations  14.2 us (2%)
    pallas_call x2, Pallas kernels, attention(): pl.pallas_call(functools.partial(attention_kernel, first, chunks, width,...  230 us
    pallas_call x2, Pallas kernels, mlp(): pl.pallas_call(functools.partial(mlp_kernel, first, layer, chunks), name=...  217 us
    all_gather x4, waiting for transfers between devices, whole(): return lax.all_gather(part, ('model', 'resp'), axis=0, tiled=True)  120 us
    unnamed x17, local copies, waits for them, and re-layouts  104 us
    pallas_call x1, Pallas kernels, head(): pl.pallas_call(functools.partial(head_kernel, chunks, tiles), name=f'head...  78.4 us
  transfers between devices with their start and end apart: 4, of which 2 were waited for; matrix products, arithmetic and copies ran while one was open for 15% of the time, Pallas kernels for 45%

profile of v1, /device:TPU:97, one launch (start us, length us, event | category | flops | bytes accessed | tf_op | source)
XLA Modules:
  0.0 799.3 jit_solution(11652079550363539772)
XLA Ops:
  6.5 0.0 all-gather.11.cloned.1.call-start
  6.6 10.8 %fusion.1 = (bf16[1,1376,2048]{2,1,0:T(8,128)(2,1)}, bf16[1,1376,2048]{2,1,0:T(8,128)(2,1)}) fusion(bf16[2,1376,2048]{2,1,0:T(8,128)(2,1)} %param.27), kind=kLoop, calls=%fused_computation.19 | loop fusion | bytes 22544384 | tf_op jit(solution)/shard_map/slice | solution.py:646
  17.4 1.3 constant_dynamic-slice_fusion.2
  18.7 2.2 copy.35
  21.0 0.1 all-gather.11.cloned.1.call-update
  21.0 0.1 all-gather.13.cloned.1.call-start
  21.1 1.3 constant_dynamic-slice_fusion
  22.4 2.3 copy.37
  24.7 0.1 all-gather.13.cloned.1.call-update
  24.8 0.1 all-gather.7.cloned.1.call-start
  24.9 2.6 fusion.2
  27.5 0.7 constant_dynamic-slice_fusion.3
  28.2 0.1 all-gather.7.cloned.1.call-update
  28.3 0.2 all-gather.9.cloned.1.call-start
  28.5 0.7 constant_dynamic-slice_fusion.1
  29.3 0.1 all-gather.9.cloned.1.call-update
  29.4 3.0 fusion.5
  32.4 1.7 copy.51
  34.1 15.1 %copy.27.refs_6_.refs_5_ = bf16[2,2048,1376]{2,1,0:T(8,128)(2,1)} copy(bf16[2,2048,1376]{1,2,0:T(8,128)(2,1)} %param.25) | data formatting | bytes 22544384 | tf_op args[10]
  49.2 15.5 %copy.28.refs_7_.refs_6_ = bf16[2,2048,1376]{2,1,0:T(8,128)(2,1)} copy(bf16[2,2048,1376]{1,2,0:T(8,128)(2,1)} %param.26) | data formatting | bytes 22544384 | tf_op args[11]
  64.7 1.7 copy.50
  67.0 0.0 copy-start
  67.0 2.4 fusion
  69.4 1.5 pad_maximum_fusion
  70.8 0.0 copy-done
  70.8 0.0 copy-start.1
  70.8 1.5 fusion.4
  72.3 0.7 copy-done.1
  73.0 1.5 fusion.3
  74.5 0.0 copy-done.2
  74.5 0.6 fusion.7
  75.1 0.0 copy-done.3
  75.1 0.6 fusion.6
  75.7 2.8 copy_bitcast_fusion.3
  78.5 2.8 copy_bitcast_fusion
  81.3 109.5 %attention0.1.refs_0_ = bf16[5,64,2048]{2,1,0:T(8,128)(2,1)} custom-call(bf16[256,2048]{1,0:T(8,128)(2,1)} %refs_1_.3, bf16[1,1024,2048]{2,1,0:T(8,128)(2,1)} %refs_2_.1, f32[1,2048]{1,0:T(1,128)} %get-tuple-element.22.refs_2_, bf16[2048,512]{1,0:T(8,128)(2,1)} %bitcast.43, bf16[2048,512]{1,0:T(8,128)(2,1)} %get-tuple-element.29.refs_4_, ...), custom_call_target="tpu_custom_call" | custom-call | flops 30000001024 | bytes 20000000 | tf_op jit(solution)/shard_map/attention0/pallas_call | solution.py:347
  190.8 0.0 all-gather.11.cloned.1.call-done
  190.8 31.6 %copy.32 = bf16[1,5504,2048]{2,1,0:T(8,128)(2,1)} copy(bf16[1,5504,2048]{2,0,1:T(2,128)(2,1)} %all-gather.11.cloned.1.call-done) | data formatting | bytes 45088768
  222.5 102.8 %all-gather.13.cloned.1.call-done = bf16[1,5504,2048]{2,0,1:T(2,128)(2,1)} async-done(((bf16[1,172,2048]{2,0,1:T(2,128)(2,1)}), bf16[1,5504,2048]{2,0,1:T(2,128)(2,1)}) %all-gather.13.cloned.1.call-update) | async-done | bytes 22544400 | tf_op jit(solution)/shard_map/all_gather | solution.py:629
  325.3 31.8 %copy.33 = bf16[1,5504,2048]{2,1,0:T(8,128)(2,1)} copy(bf16[1,5504,2048]{2,0,1:T(2,128)(2,1)} %all-gather.13.cloned.1.call-done) | data formatting | bytes 45088768
  357.1 16.8 %all-gather.7.cloned.1.call-done.refs_5_ = bf16[2048,2048]{1,0:T(8,128)(2,1)} async-done(((bf16[64,2048]{1,0:T(8,128)(2,1)}), bf16[2048,2048]{1,0:T(8,128)(2,1)}) %all-gather.7.cloned.1.call-update) | async-done | bytes 8388624 | tf_op jit(solution)/shard_map/all_gather | solution.py:629
  373.8 126.7 %mlp1.1 = (bf16[5,64,2048]{2,1,0:T(8,128)(2,1)}, bf16[5,64,2048]{2,1,0:T(8,128)(2,1)}) custom-call(bf16[5,64,2048]{2,1,0:T(8,128)(2,1)} %attention0.1.refs_0_, bf16[256,2048]{1,0:T(8,128)(2,1)} %refs_1_.3, bf16[1,1024,2048]{2,1,0:T(8,128)(2,1)} %refs_2_.1, f32[1,2048]{1,0:T(1,128)} %get-tuple-element.20.refs_3_, f32[1,2048]{1,0:T(1,128)} %get-tuple-element.21.refs_4_, ...), custom_call_target="tpu_custom_call" | custom-call | flops 80000000000 | bytes 50000000 | tf_op jit(solution)/shard_map/mlp1/pallas_call | solution.py:476
  500.5 120.5 %attention2.1.refs_0_ = bf16[4,64,2048]{2,1,0:T(8,128)(2,1)} custom-call(bf16[5,64,2048]{2,1,0:T(8,128)(2,1)} %get-tuple-element.7.refs_0_, bf16[2048,512]{1,0:T(8,128)(2,1)} %bitcast.42, bf16[2048,512]{1,0:T(8,128)(2,1)} %get-tuple-element.31.refs_2_, bf16[2048,512]{1,0:T(8,128)(2,1)} %get-tuple-element.30.refs_3_, ...), custom_call_target="tpu_custom_call" | custom-call | flops 30000001024 | bytes 20000000 | tf_op jit(solution)/shard_map/attention2/pallas_call | solution.py:347
  621.0 0.0 all-gather.9.cloned.1.call-done.refs_4_
  621.0 90.2 %mlp3.1.h_in = bf16[4,64,2048]{2,1,0:T(8,128)(2,1)} custom-call(bf16[4,64,2048]{2,1,0:T(8,128)(2,1)} %attention2.1.refs_0_, bf16[5,64,2048]{2,1,0:T(8,128)(2,1)} %get-tuple-element.8.refs_1_, f32[1,2048]{1,0:T(1,128)} %get-tuple-element.19.refs_2_, f32[1,2048]{1,0:T(1,128)} %bitcast.45, bf16[2048,2048]{1,0:T(8,128)(2,1)} %all-gather.9.cloned.1.call-done.refs_4_, ...), custom_call_target="tpu_custom_call" | custom-call | flops 80000000000 | bytes 50000000 | tf_op jit(solution)/shard_map/mlp3/pallas_call | solution.py:476
  711.2 1.7 broadcast_in_dim.14.target
  712.9 78.4 %head4.1 = f32[1,1024]{1,0:T(1,128)} custom-call(bf16[4,64,2048]{2,1,0:T(8,128)(2,1)} %mlp3.1.h_in, bf16[2048,8192]{1,0:T(8,128)(2,1)} %wv.1, s32[1024,128]{1,0:T(8,128)} %broadcast_in_dim.14.target, s32[1]{0:T(128)S(6)} %copy.53.lens), custom_call_target="tpu_custom_call" | custom-call | flops 40000000000 | bytes 50000000 | tf_op jit(solution)/shard_map/head4/pallas_call | solution.py:592
  791.3 1.3 copy.54
  (6 shorter events, 0.0 us)
Async XLA Ops:
  6.5 184.3 %all-gather.11.cloned.1.call-start = ((), (), s32[]{:S(2)}) async-start(), calls=%async_computation.2 | async-start | bytes 46497792 | tf_op jit(solution)/shard_map/all_gather | solution.py:629
  21.0 304.2 %all-gather.13.cloned.1.call-start = ((), (), s32[]{:S(2)}) async-start(), calls=%async_computation.3 | async-start | bytes 46497792 | tf_op jit(solution)/shard_map/all_gather | solution.py:629
  24.8 349.0 %all-gather.7.cloned.1.call-start = ((), (), s32[]{:S(2)}) async-start(), calls=%async_computation | async-start | bytes 8650752 | tf_op jit(solution)/shard_map/all_gather | solution.py:629
  28.3 592.7 %all-gather.9.cloned.1.call-start = ((), (), s32[]{:S(2)}) async-start(), calls=%async_computation.1 | async-start | bytes 8650752 | tf_op jit(solution)/shard_map/all_gather | solution.py:629
  67.0 3.8 copy-start
  70.8 2.2 copy-start.1
  73.0 1.5 copy-start.2
  73.0 2.1 copy-start.3
Sparse Core Ops, SparseCore 0:
  21.1 164.2 all-gather.10
  187.5 137.7 all-gather.12
  327.3 46.4 all-gather.6
  375.8 65.4 all-gather.8

commit v2 on v0

v2 whole, which is shorter than its diff:
```python
import functools

import jax
import jax.numpy as jnp
from jax import lax
from jax.experimental import pallas as pl
from jax.experimental.pallas import tpu as pltpu
from jax.sharding import PartitionSpec as P

EPS = 1e-6
ROPE_BASE = 10000.0
LOG2E = 1.4426950408889634
VMEM_BYTES = 67043328
ROWS = 64
LANES = 128
BLOCK = 256
BF = jnp.bfloat16
F32 = jnp.float32
ANY = pl.BlockSpec(memory_space=pl.ANY)
VM = pl.BlockSpec(memory_space=pltpu.VMEM)
MESH = pl.DeviceIdType.MESH
RIGHT, LEFT, RIGHT_ON, LEFT_ON, OWN_MATE, LEFT_MATE, RIGHT_MATE, OPP_MATE = range(8)


def ds(index, size):
    return pl.ds(pl.multiple_of(index * size, size), size)


def dot(a, b):
    return jnp.dot(a, b, preferred_element_type=F32)


def dot_t(a, b):
    return lax.dot_general(a, b, (((1,), (1,)), ((), ())), preferred_element_type=F32)


def sems(*shape):
    return pltpu.SemaphoreType.DMA(shape)


def remote(src, dst, send, recv, axis, where):
    return pltpu.make_async_remote_copy(src_ref=src, dst_ref=dst, send_sem=send, recv_sem=recv, device_id={axis: where}, device_id_type=MESH)


def local(src, dst, sem):
    copy = pltpu.make_async_copy(src, dst, sem)
    copy.start()
    return copy


def greet(rings):
    barrier = pltpu.get_barrier_semaphore()
    peers = {}
    for ring in rings:
        for i, where in enumerate(ring.places[1:]):
            peers[ring.axis, i] = (ring.axis, where)
        if ring.mate is not None:
            peers['mate'] = (ring.axis, ring.mate)
    for axis, where in peers.values():
        pl.semaphore_signal(barrier, inc=1, device_id={axis: where}, device_id_type=MESH)
    pl.semaphore_wait(barrier, len(peers))


class Ring:
    def __init__(self, axis, me, stride, piece, send, recv, source=None, mate=None):
        self.axis, self.piece, self.send, self.recv, self.source, self.mate = axis, piece, send, recv, source, mate
        self.places = [lax.rem(me + k * stride, 4 * stride) for k in range(4)]
        self.own, self.right, self.opp, self.left = self.places
        self.mate_step = None if mate is None else mate - me

    def copy(self, kind, u, owner, source=None):
        dst = self.piece(u, owner)
        if kind in (RIGHT_ON, LEFT_ON):
            half = dst.shape[0] // 2
            dst = dst.at[pl.ds((kind - RIGHT_ON) * half, half)]
        where = self.mate if kind >= OWN_MATE else self.left if kind in (LEFT, LEFT_ON) else self.right
        return remote(dst if source is None else source, dst, self.send.at[kind, u], self.recv.at[kind, u], self.axis, where)

    def start(self, u):
        for kind in (OWN_MATE, RIGHT, LEFT)[self.mate is None:]:
            self.copy(kind, u, self.own, self.source and self.source(u)).start()

    def forward(self, u):
        for kind, owner in ((RIGHT, self.left), (LEFT, self.right)):
            self.copy(kind, u, owner).wait_recv()
            self.copy(kind + RIGHT_ON, u, owner).start()
            if self.mate is not None:
                self.copy(kind + LEFT_MATE, u, owner).start()

    def finish(self, u):
        for kind in (RIGHT_ON, LEFT_ON):
            self.copy(kind, u, self.opp).wait_recv()
        if self.mate is not None:
            self.copy(OPP_MATE, u, self.opp).start()

    def mate_arrived(self, u):
        for kind, owner in ((OWN_MATE, self.own), (LEFT_MATE, self.left), (RIGHT_MATE, self.right), (OPP_MATE, self.opp)):
            self.copy(kind, u, owner + self.mate_step).wait_recv()

    def drain(self, u):
        for kind, owner in ((RIGHT, self.own), (LEFT, self.own), (RIGHT_ON, self.left), (LEFT_ON, self.right), (OWN_MATE, self.own), (LEFT_MATE, self.left), (RIGHT_MATE, self.right), (OPP_MATE, self.opp)):
            if kind < OWN_MATE or self.mate is not None:
                self.copy(kind, u, owner).wait_send()


def resp_ring(piece, send, recv, source=None):
    r = lax.axis_index('resp')
    return Ring('resp', r, 2, piece, send, recv, source, r + 1 - 2 * lax.rem(r, 2))


def model_ring(piece, send, recv, source=None):
    return Ring('model', lax.axis_index('model'), 1, piece, send, recv, source)


def norm_rows(src, dst, gain_ref, rows, width):
    def square(n, total):
        block = src(ds(n, BLOCK)).astype(F32)
        sq = block * block
        return total + sq[:, :LANES] + sq[:, LANES:]

    trips = width // BLOCK
    total = lax.fori_loop(0, trips, square, jnp.zeros((rows, LANES), F32), unroll=2)
    inv = lax.rsqrt(jnp.sum(total, axis=-1, keepdims=True) / width + EPS)

    def scale(n, carry):
        cols = ds(n, BLOCK)
        dst(cols, (src(cols).astype(F32) * inv * gain_ref[:, cols]).astype(BF))
        return carry

    lax.fori_loop(0, trips, scale, 0, unroll=2)


def loop(lo, hi, body):
    def wrapped(i, carry):
        body(i)
        return carry
    lax.fori_loop(lo, hi, wrapped, 0)


def when(condition, *actions):
    @pl.when(condition)
    def _():
        for action in actions:
            action()


def params(collective):
    return pltpu.CompilerParams(collective_id=collective, has_side_effects=True, vmem_limit_bytes=VMEM_BYTES)


def work(flops):
    return pl.CostEstimate(flops=flops, bytes_accessed=flops // 1000, transcendentals=0)


def attention_kernel(first, layer, chunks, *refs):
    if first:
        xp, xr, gain, *refs = refs
    else:
        hin, *refs = refs
    wq, wk, wv, cos, sin, w_out, w_down, o_out, wo_all, wo_y, wd_y, *refs = refs
    if first:
        x_v, *refs = refs
    h_v, q_v, k_v, v_v, acc_v, m_v, l_v, o_v, load, h_s, h_r, kv_s, kv_r, y_s, y_r, wo_s, wo_r, o_s, o_r, own_s = refs
    me, r = lax.axis_index('model'), lax.axis_index('resp')
    chip = r // 2
    width = wq.shape[-1]
    dim = wq.shape[0]
    heads = width // LANES
    log_scale = LOG2E * LANES ** -0.5
    prompt_blocks = k_v.shape[0] - (chunks - 1)

    gather = model_ring(lambda c, b: h_v.at[c, b], h_s, h_r)
    kv = resp_ring(lambda u, b: (k_v, v_v)[u].at[b], kv_s, kv_r)
    ours = ds(r, BLOCK)
    spread = model_ring(lambda u, b: (wo_y, wd_y)[u].at[b], y_s, y_r, lambda u: (w_out, w_down)[u].at[layer, :, ours])
    shares = spread.places[1:]
    outs = resp_ring(lambda u, b: wo_all.at[shares[u], :, ds(b, BLOCK)], wo_s, wo_r, lambda u: wo_y.at[shares[u]])

    if first:
        loads = [local(xp, x_v.at[0], load.at[0])] + [local(xr.at[0, pl.ds((c - 1) * BLOCK, BLOCK)], x_v.at[c], load.at[c]) for c in range(1, chunks)]
    else:
        loads = [local(hin.at[c], h_v.at[c, me], load.at[c]) for c in range(chunks)]
    greet([gather, kv])
    own_cols = []

    def spread_done(u):
        spread.finish(u)
        if u == 0:
            for s in range(3):
                outs.start(s)
                own_cols.append(local(wo_y.at[shares[s]], wo_all.at[shares[s], :, ours], own_s.at[s]))

    def key_block(c):
        return jnp.where(c == 0, r, prompt_blocks + c - 1)

    def project(c):
        rows = pl.ds(pl.multiple_of(c * BLOCK, BLOCK), BLOCK)
        cs, sn = cos[rows, :], sin[rows, :]
        blk = key_block(c)
        for which, w in enumerate((wk, wv, wq)):
            for n in range(width // BLOCK):
                y = dot(h_v[c].reshape(BLOCK, dim), w[:, pl.ds(n * BLOCK, BLOCK)])
                for i in range(2):
                    cols = pl.ds((2 * n + i) * LANES, LANES)
                    part = y[:, i * LANES:(i + 1) * LANES]
                    if which == 1:
                        v_v[blk, cols, :] = part.T.astype(BF)
                    else:
                        part = (part * cs + pltpu.roll(part, LANES // 2, 1) * sn).astype(BF)
                        if which == 2:
                            q_v[c, :, cols] = part
                        else:
                            k_v[blk, :, cols] = part

    kv_units = range(2)

    def kv_do(name):
        for u in kv_units:
            getattr(kv, name)(u)

    if first:
        spread.start(0)
        spread.start(1)

        def chunk(c):
            norm_rows(lambda cols: x_v[c, :, cols], lambda cols, val: h_v.__setitem__((c, slice(None), slice(None), cols), val.reshape(4, ROWS, BLOCK)), gain, BLOCK, dim)
            project(c)
            when(c == 0, lambda: kv_do('start'))
            when(c == 2, lambda: spread.forward(0))

        for cp in loads:
            cp.wait()
        loop(0, chunks, chunk)
    else:
        for c in range(2):
            loads[c].wait()
            gather.start(c)
        for cp in loads[2:]:
            cp.wait()

        def chunk(c):
            def receive():
                gather.forward(c)
                when(c + 2 < chunks, lambda: gather.start(c + 2))
            when(c < chunks, receive)

            def use():
                gather.finish(c - 1)
                project(c - 1)
            when(c > 0, use)
            when(c == 1, lambda: kv_do('start'))
            when(c == chunks - 1, lambda: kv_do('forward'))

        loop(0, chunks + 1, chunk)
        spread.start(0)
        spread.start(1)

    key_i = lax.broadcasted_iota(jnp.int32, (BLOCK, BLOCK), 0)
    causal = key_i <= lax.broadcasted_iota(jnp.int32, (BLOCK, BLOCK), 1)

    def step(qi, kb, blocks, diagonal=False):
        def scores(n):
            cols = pl.ds(n * LANES, LANES)
            s = dot_t(k_v[pl.ds(kb, blocks), :, cols].reshape(blocks * BLOCK, LANES), q_v[qi, :, cols])
            return jnp.where(causal, s, -jnp.inf) if diagonal else s

        ahead = scores(0)
        for n in range(heads):
            s = ahead
            if n + 1 < heads:
                ahead = scores(n + 1)
            top = jnp.max(s, axis=0, keepdims=True)
            if not diagonal:
                m = m_v[qi, n, :1]
                top = jnp.maximum(m, top)
            p = jnp.exp2((s - top) * log_scale)
            total = jnp.sum(p, axis=0, keepdims=True)
            p = p.astype(BF)
            mixed = None
            for b in range(blocks):
                part = dot(v_v[kb + b, pl.ds(n * LANES, LANES), :], p[b * BLOCK:(b + 1) * BLOCK])
                mixed = part if mixed is None else mixed + part
            if not diagonal:
                alpha = jnp.exp2((m - top) * log_scale)
                total = total + l_v[qi, n, :1] * alpha
                mixed = mixed + acc_v[qi, n] * alpha
            m_v[qi, n, :1] = top
            l_v[qi, n, :1] = total
            acc_v[qi, n] = mixed

    low = 0 if first else 1

    def own(qi):
        step(qi, key_block(qi), 1, True)
        loop(prompt_blocks, prompt_blocks + qi - 1, lambda b: step(qi, b, 1))

    loop(low, chunks, own)

    if first:
        spread_done(0)
        kv_do('forward')
        spread.forward(1)
    kv_do('finish')
    kv_do('mate_arrived')
    if not first:
        spread.forward(0)

    def o_copy(c, k):
        owner = spread.places[k]
        return remote(o_v.at[c, owner], o_out.at[c, :, ds(me, width)], o_s.at[k - 1, c], o_r.at[k - 1, c], 'model', owner)

    def o_own(c):
        return pltpu.make_async_copy(o_v.at[c, me], o_out.at[c, :, ds(me, width)], load.at[c])

    def prompt(qi):
        c = qi - low
        loop(0, jnp.where(qi == 0, chip, 4), lambda x: step(qi, 2 * x, 2))
        when((qi == 0) & (r > 2 * chip), lambda: step(qi, 2 * chip, 1))
        for n in range(heads):
            out = (acc_v[qi, n] / l_v[qi, n, :1]).T.astype(BF)
            o_v[c, :, :, pl.ds(n * LANES, LANES)] = out.reshape(4, ROWS, LANES)
        for k in (2, 1, 3):
            o_copy(c, k).start()
        o_own(c).start()

    events = [lambda: outs.forward(0), lambda: outs.forward(1), lambda: (outs.forward(2), outs.finish(0)), lambda: outs.finish(1)]
    if not first:
        events = []

    def prompt_and_events(qi):
        prompt(qi)
        for i, event in enumerate(events):
            when(qi == i + low, event)

    loop(low, chunks, prompt_and_events)
    if first:
        spread_done(1)
        outs.finish(2)
    else:
        spread_done(0)
        spread.forward(1)
        for s in range(3):
            outs.forward(s)
        for s in range(3):
            outs.finish(s)
        spread_done(1)
    for s in range(3):
        outs.mate_arrived(s)
        outs.drain(s)
        own_cols[s].wait()
    for u in kv_units:
        kv.drain(u)
        spread.drain(u)
    for c in range(chunks - low):
        for k in (1, 2, 3):
            o_copy(c, k).wait()
        o_own(c).wait()
    if not first:
        for c in range(chunks):
            gather.drain(c)


def attention(first, layer, collective, hidden, gain, wq, wk, wv, cos, sin, w_out, w_down):
    dim, width = wq.shape
    chunks = cos.shape[0] // BLOCK
    outs = chunks if first else chunks - 1
    heads = width // LANES
    blocks = lax.psum(1, 'resp') + chunks - 1
    args = hidden + ((gain,) if first else ()) + (wq, wk, wv, cos, sin, w_out, w_down)
    specs = [ANY] * len(hidden) + [VM] * (len(args) - len(hidden) - 2) + [ANY] * 2
    ffn = w_down.shape[1]
    shapes = [(outs, ROWS, 4 * width), (4, width, dim), (4, width, BLOCK), (4, ffn, BLOCK)]
    scratch = [pltpu.VMEM((chunks, BLOCK, dim), BF)] if first else []
    state = pltpu.VMEM((chunks, heads, 8, BLOCK), F32)
    scratch += [
        pltpu.VMEM((chunks, 4, ROWS, dim), BF),
        pltpu.VMEM((chunks, BLOCK, width), BF),
        pltpu.VMEM((blocks, BLOCK, width), BF),
        pltpu.VMEM((blocks, width, BLOCK), BF),
        pltpu.VMEM((chunks, heads, LANES, BLOCK), F32),
        state,
        state,
        pltpu.VMEM((outs, 4, ROWS, width), BF),
        sems(chunks),
    ]
    for kinds, units in ((4, chunks), (8, 2), (4, 2), (8, 3), (3, outs)):
        scratch += [sems(kinds, units)] * 2
    scratch.append(sems(3))
    return pl.pallas_call(
        functools.partial(attention_kernel, first, layer, chunks),
        name=f'attention{layer}',
        out_shape=tuple(jax.ShapeDtypeStruct(s, BF) for s in shapes),
        in_specs=specs,
        out_specs=(ANY,) * len(shapes),
        scratch_shapes=scratch,
        compiler_params=params(collective),
        cost_estimate=work(30_000_000_000),
    )(*args)


def mlp_kernel(first, layer, chunks, *refs):
    o_in, *rows_in, gain, next_gain, w_out, wo_all, wg, wu, w_down, wd_y, h_out = refs[:12 if first else 11]
    refs = refs[12 if first else 11:]
    if first:
        x_out, *refs = refs
    wo_v, wg_v, wu_v, wd_v, o_v, x_v, u_v, si_v, ri_v, load, wl, wd_l, h_s, h_r, x_s, x_r, i_s, i_r = refs
    me, r = lax.axis_index('model'), lax.axis_index('resp')
    dim = x_v.shape[-1]
    ffn = wg_v.shape[0]
    width = wo_v.shape[1]
    rows = chunks * ROWS
    gather = model_ring(lambda c, b: u_v.at[c, b], h_s, h_r)
    shares = gather.places[1:]
    downs = resp_ring(lambda u, b: wd_v.at[u + 1, :, ds(b, BLOCK)], x_s, x_r, lambda u: wd_y.at[shares[u]])

    start = [local(o_in, o_v, load.at[0]), local(w_out.at[layer], wo_v.at[me], wl.at[0])]
    start += [local(wo_all.at[s], wo_v.at[s], wl.at[i]) for i, s in enumerate(shares, 1)]
    if first:
        start += [local(rows_in[0].at[ds(me, ROWS)], x_v.at[0], load.at[1])]
        start += [local(rows_in[1].at[0, ds((c - 1) * 4 + me, ROWS)], x_v.at[c], load.at[1 + c]) for c in range(1, chunks)]
    else:
        start += [local(rows_in[0].at[pl.ds(1, chunks)], x_v, load.at[1])]
    weights = [local(wg.at[layer], wg_v, wl.at[4]), local(wu.at[layer], wu_v, wl.at[5])]
    greet([gather, downs])
    for u in range(3):
        downs.start(u)
    kept = [local(w_down.at[layer], wd_v.at[0], wd_l.at[0])]
    kept += [local(wd_y.at[s], wd_v.at[i, :, ds(r, BLOCK)], wd_l.at[i]) for i, s in enumerate(shares, 1)]
    for cp in start:
        cp.wait()

    def outproj(n):
        cols = ds(n, 2 * BLOCK)
        y = dot(o_v[...].reshape(rows, dim), wo_v[:, :, cols].reshape(dim, 2 * BLOCK))
        x_v[:, :, cols] = (x_v[:, :, cols].reshape(rows, 2 * BLOCK).astype(F32) + y).astype(BF).reshape(chunks, ROWS, 2 * BLOCK)

    loop(0, dim // (2 * BLOCK), outproj)

    def normalize(c):
        norm_rows(lambda cols: x_v[c, :, cols], lambda cols, val: u_v.__setitem__((c, me, slice(None), cols), val), gain, ROWS, dim)
        when(c < 2, lambda: gather.start(c))

    loop(0, chunks, normalize)
    for cp in weights:
        cp.wait()

    def i_send(c, k):
        return remote(si_v.at[c, gather.places[k]], ri_v.at[3 - k, c], i_s.at[k - 1, c], i_r.at[k - 1, c], 'model', gather.places[k])

    def i_recv(c, q):
        ref = ri_v.at[q - 1, c]
        return remote(ref, ref, i_s.at[3 - q, c], i_r.at[3 - q, c], 'model', gather.places[q])

    def gate_up(c):
        lhs = u_v[c].reshape(4 * ROWS, dim)
        half = ffn // 2
        for lo in (0, half):
            cols = pl.ds(lo, half)
            g = dot_t(lhs, wg_v[cols, :])
            inner = (g * jax.nn.sigmoid(g) * dot_t(lhs, wu_v[cols, :])).astype(BF)
            si_v[c, :, :, cols] = inner.reshape(4, ROWS, half)
        for k in (2, 1, 3):
            i_send(c, k).start()

    events = {2: lambda: downs.forward(0), 3: lambda: downs.forward(1), 4: lambda: (downs.forward(2), downs.finish(0))}

    def chunk(c):
        def receive():
            gather.forward(c)
            when(c + 2 < chunks, lambda: gather.start(c + 2))
        when(c < chunks, receive)

        def use():
            gather.finish(c - 1)
            gate_up(c - 1)
        when(c > 0, use)
        for at, event in events.items():
            when(c == at, event)

    loop(0, chunks + 1, chunk)
    downs.finish(1)
    downs.finish(2)
    for u in range(3):
        downs.mate_arrived(u)
    for cp in kept:
        cp.wait()

    def down(lo, hi):
        size = hi - lo

        def tile(n):
            cols = ds(n, BLOCK)
            y = dot(si_v[lo:hi, me].reshape(size * ROWS, ffn), wd_v[0, :, cols])
            for q in (1, 2, 3):
                y = y + dot(ri_v[q - 1, lo:hi].reshape(size * ROWS, ffn), wd_v[q, :, cols])
            x_v[lo:hi, :, cols] = (x_v[lo:hi, :, cols].reshape(size * ROWS, BLOCK).astype(F32) + y).astype(BF).reshape(size, ROWS, BLOCK)

        loop(0, dim // BLOCK, tile)
        loop(lo, hi, lambda c: norm_rows(lambda cols: x_v[c, :, cols], lambda cols, val: o_v.__setitem__((c, slice(None), cols), val), next_gain, ROWS, dim))

    split = (chunks + 1) // 2
    stored = []
    for part, (lo, hi) in enumerate(((0, split), (split, chunks))):
        for c in range(lo, hi):
            for q in (1, 2, 3):
                i_recv(c, q).wait_recv()
        down(lo, hi)
        span = pl.ds(lo, hi - lo)
        stored.append(local(o_v.at[span], h_out.at[span], load.at[part]))
        if first:
            stored.append(local(x_v.at[span], x_out.at[span], load.at[2 + part]))
    for cp in stored:
        cp.wait()
    for u in range(3):
        downs.drain(u)
    for c in range(chunks):
        gather.drain(c)
        for k in (1, 2, 3):
            i_send(c, k).wait_send()


def mlp(first, layer, collective, o_in, rows_in, gain, next_gain, w_out, wo_all, wg, wu, w_down, wd_y):
    chunks, _, dim = o_in.shape
    ffn = wg.shape[1]
    args = (o_in, *rows_in, gain, next_gain, w_out, wo_all, wg, wu, w_down, wd_y)
    specs = [ANY] * (1 + len(rows_in)) + [VM] * 2 + [ANY] * 6
    count = 2 if first else 1
    scratch = [pltpu.VMEM(s, BF) for s in (wo_all.shape, (ffn, dim), (ffn, dim), (4, ffn, dim), (chunks, ROWS, dim), (chunks, ROWS, dim), (chunks, 4, ROWS, dim), (chunks, 4, ROWS, ffn), (3, chunks, ROWS, ffn))]
    scratch += [sems(6), sems(6), sems(4)]
    for kinds, units in ((4, chunks), (8, 3), (3, chunks)):
        scratch += [sems(kinds, units)] * 2
    return pl.pallas_call(
        functools.partial(mlp_kernel, first, layer, chunks),
        name=f'mlp{layer}',
        out_shape=(jax.ShapeDtypeStruct((chunks, ROWS, dim), BF),) * count,
        in_specs=specs,
        out_specs=(ANY,) * count,
        scratch_shapes=scratch,
        compiler_params=params(collective),
        cost_estimate=work(80_000_000_000),
    )(*args)


def head_kernel(chunks, tiles, h_in, wv, target, lens, out, wv_v, u_v, m_v, l_v, p_v, st_v, load, wl, h_s, h_r, st_s, st_r):
    me = lax.axis_index('model')
    dim, vocab = wv_v.shape
    span = vocab // tiles
    tile = 4 * BLOCK
    gather = model_ring(lambda c, b: u_v.at[c, b], h_s, h_r)
    rows = [local(h_in.at[c], u_v.at[c, me], load.at[c]) for c in range(chunks)]

    def weight(t):
        cols = ds(t, span)
        return pltpu.make_async_copy(wv.at[:, cols], wv_v.at[:, cols], wl.at[t])

    loop(0, tiles, lambda t: weight(t).start())
    greet([gather])
    for cp in rows:
        cp.wait()
    for c in range(2):
        gather.start(c)
    lane = lax.broadcasted_iota(jnp.int32, (BLOCK, LANES), 1)
    pieces = range(tile // LANES)

    def logits(c, n):
        s = dot(u_v[c].reshape(BLOCK, dim), wv_v[:, ds(n, tile)])
        parts = [s[:, i * LANES:(i + 1) * LANES] for i in pieces]
        m = m_v[...]
        top = functools.reduce(jnp.maximum, parts, m)
        total = l_v[...] * jnp.exp2((m - top) * LOG2E)
        picked = p_v[...]
        wanted = target[ds(c, BLOCK), :] - me * vocab - n * tile
        for i in pieces:
            total = total + jnp.exp2((parts[i] - top) * LOG2E)
            picked = picked + jnp.where(wanted - i * LANES == lane, parts[i], 0.0)
        m_v[...] = top
        l_v[...] = total
        p_v[...] = picked

    def vocab_pass(c):
        m_v[...] = jnp.full_like(m_v, -jnp.inf)
        l_v[...] = jnp.zeros_like(l_v)
        p_v[...] = jnp.zeros_like(p_v)
        per = span // tile

        def columns(n):
            when((c == 0) & (lax.rem(n, per) == 0), lambda: weight(n // per).wait())
            logits(c, n)

        loop(0, vocab // tile, columns)
        m = m_v[...]
        top = jnp.max(m, axis=-1, keepdims=True)
        total = jnp.sum(l_v[...] * jnp.exp2((m - top) * LOG2E), axis=-1, keepdims=True)
        picked = jnp.sum(p_v[...], axis=-1, keepdims=True)
        stat = jnp.where(lane == 0, top, jnp.where(lane == 1, total, picked))
        st_v[me, :, ds(c, BLOCK)] = stat.T[:8]

    def chunk(c):
        def receive():
            gather.forward(c)
            when(c + 2 < chunks, lambda: gather.start(c + 2))
        when(c < chunks, receive)

        def use():
            gather.finish(c - 1)
            vocab_pass(c - 1)
        when(c > 0, use)

    loop(0, chunks + 1, chunk)

    def st_copy(k, block):
        return remote(st_v.at[block], st_v.at[block], st_s.at[k - 1], st_r.at[k - 1], 'model', gather.places[k])

    for k in (2, 1, 3):
        st_copy(k, me).start()
    for k in (1, 2, 3):
        st_copy(k, gather.places[4 - k]).wait_recv()
    tops = [st_v[s, 0:1, :] for s in range(4)]
    top = functools.reduce(jnp.maximum, tops)
    total = sum(st_v[s, 1:2, :] * jnp.exp2((tops[s] - top) * LOG2E) for s in range(4))
    value = sum(st_v[s, 2:3, :] for s in range(4)) - top - jnp.log(total)
    token = lax.broadcasted_iota(jnp.int32, value.shape, 1)
    out[...] = jnp.where(token < lens[0], value, 0.0)
    for k in (1, 2, 3):
        st_copy(k, me).wait_send()
    for c in range(chunks):
        gather.drain(c)


def head(collective, h_in, wv, target, lens):
    chunks, _, dim = h_in.shape
    tiles = 4
    stat = pltpu.VMEM((BLOCK, LANES), F32)
    return pl.pallas_call(
        functools.partial(head_kernel, chunks, tiles),
        name='head',
        out_shape=jax.ShapeDtypeStruct((1, chunks * BLOCK), F32),
        in_specs=[ANY, ANY, VM, pl.BlockSpec(memory_space=pltpu.SMEM)],
        out_specs=VM,
        scratch_shapes=[
            pltpu.VMEM(wv.shape, BF),
            pltpu.VMEM((chunks, 4, ROWS, dim), BF),
            stat,
            stat,
            stat,
            pltpu.VMEM((4, 8, chunks * BLOCK), F32),
            sems(chunks),
            sems(tiles),
        ] + [sems(4, chunks)] * 2 + [sems(3)] * 2,
        compiler_params=params(collective),
        cost_estimate=work(40_000_000_000),
    )(h_in, wv, target, lens)


def rope_tables(prompt_rows, resp_len, groups):
    half = LANES // 2
    freq = ROPE_BASE ** (-jnp.arange(half, dtype=F32) / half)
    pos = jnp.concatenate([lax.axis_index('resp') * prompt_rows + jnp.arange(prompt_rows), prompt_rows * groups + jnp.arange(resp_len)])
    angles = pos.astype(F32)[:, None] * freq
    c, s = jnp.cos(angles), jnp.sin(angles)
    return jnp.concatenate([c, c], axis=-1), jnp.concatenate([-s, s], axis=-1)


def solution(mesh):
    groups = mesh.shape['resp']
    row_axes = ('prompts', 'resp')
    head_spec = P(None, None, 'model', None)
    in_specs = (P(row_axes, None), P(row_axes, None, None), P(row_axes, None), P(row_axes), P(None, None), head_spec, head_spec, head_spec, P(None, 'model', None, None), P(None, None), P(None, None, 'model'), P(None, None, 'model'), P(None, 'model', None), P(None), P(None, 'model'))

    def device_step(x_prompt, x_resp, targets, resp_lens, attn_gain, w_query, w_key, w_value, w_out, mlp_gain, w_gate, w_up, w_down, final_gain, w_vocab):
        layers, dim, heads, head_dim = w_query.shape
        width = heads * head_dim
        resp_len = x_resp.shape[1]
        cos, sin = rope_tables(x_prompt.shape[0], resp_len, groups)
        flat = [[w[l].reshape(dim, width) for w in (w_query, w_key, w_value)] for l in range(layers)]
        w_out = w_out.reshape(layers, width, dim)
        gates = [jnp.swapaxes(w, 1, 2) for w in (w_gate, w_up)]
        gains = [attn_gain[l:l + 1] for l in range(layers)] + [final_gain[None, :]]
        target = jnp.broadcast_to(targets[0][:, None], (resp_len, LANES))
        rows = (x_prompt, x_resp)
        hidden = rows
        for l in range(layers):
            first = l == 0
            o, wo_all, _, wd_y = attention(first, l, 2 * l, hidden, gains[l], *flat[l], cos, sin, w_out, w_down)
            h, *rows = mlp(first, l, 2 * l + 1, o, rows, mlp_gain[l:l + 1], gains[l + 1], w_out, wo_all, *gates, w_down, wd_y)
            hidden = (h,)
        return head(2 * layers, h, w_vocab, target, resp_lens)

    return jax.shard_map(device_step, mesh=mesh, in_specs=in_specs, out_specs=P(row_axes, None), check_vma=False)
```

time: 1170 us -> 495 us (0.42)
  waiting for transfers between devices: 697 us -> 0 us
  Pallas kernels: 0 us -> 467 us
  matrix products: 281 us -> 0 us
  other arithmetic: 118 us -> 3.86 us
  between operations: 15.1 us -> 0.74 us
  blocking collectives: 13.6 us -> 0 us
    psum x4 -> x0, waiting for transfers between devices: 682 us -> none  [the longest x2 343 us: device_step(): lax.psum(attn_part, 'model')]
    pallas_call x0 -> x5, Pallas kernels: none -> 467 us  [the longest x2 200 us: attention(): pl.pallas_call(functools.partial(attention_kernel, first, layer, chunks),...]
    dot_general x12 -> x0, matrix products: 262 us -> none  [the longest x2 75.4 us: device_step(): jnp.dot(inner, w_down[layer_idx], preferred_element_type=jnp.float32)]
    reduce_sum x8 -> x0, other arithmetic: 90.2 us -> none  [the longest x2 41.4 us: attend(): row_sum = jnp.moveaxis(jnp.sum(exp_scores, axis=-1), -1, -3)]
    unnamed x4 -> x0, matrix products: 18.4 us -> none
    all_gather x4 -> x0, waiting for transfers between devices: 14.2 us -> none  [the longest x2 14.2 us: device_step(): prompt_keys = lax.all_gather(keys[:prompt_rows], 'resp', axis=0, tiled=True)]
    unnamed x64 -> x15, local copies, waits for them, and re-layouts: 18.7 us -> 5.23 us
  transfers between devices with their start and end apart: 8 -> 0, of which waited for: 6 -> 0; matrix products, arithmetic and copies ran while one was open for 11% -> 0% of each run, Pallas kernels for 0% -> 0%
where the time goes in v2:
time: 495 us; the launch traced here: 494 us
  Pallas kernels  467 us (94%)
  local copies, waits for them, and re-layouts  22.8 us (5%)
    pallas_call x2, Pallas kernels, attention(): pl.pallas_call(functools.partial(attention_kernel, first, layer, chunks),...  200 us
    pallas_call x2, Pallas kernels, mlp(): pl.pallas_call(functools.partial(mlp_kernel, first, layer, chunks), name=...  193 us
    pallas_call x1, Pallas kernels, head(): pl.pallas_call(functools.partial(head_kernel, chunks, tiles), name='head'...  74 us

profile of v2, /device:TPU:97, one launch (start us, length us, event | category | flops | bytes accessed | tf_op | source)
XLA Modules:
  0.0 494.2 jit_solution(16863703188308334920)
XLA Ops:
  0.0 0.0 copy-start.1
  0.0 2.4 fusion
  2.4 1.5 pad_maximum_fusion
  3.9 0.0 copy-done.1
  3.9 0.0 copy-start.2
  3.9 2.5 fusion.1
  6.4 0.4 copy-done.2
  6.8 2.4 fusion.2
  9.3 0.0 copy-start.4
  9.3 0.0 copy-start.5
  9.3 0.0 copy-start.3
  9.3 2.8 copy_bitcast_fusion.3
  12.1 0.0 copy-done.4
  12.1 0.0 copy-done.5
  12.1 0.6 fusion.4
  12.7 0.0 copy-done.3
  12.7 2.4 fusion.3
  15.2 1.7 copy.29
  16.9 87.6 %attention0.1 = (bf16[5,64,2048]{2,1,0:T(8,128)(2,1)}, bf16[4,512,2048]{2,1,0:T(8,128)(2,1)}, bf16[4,512,256]{2,1,0:T(8,128)(2,1)}, bf16[4,1376,256]{2,1,0:T(8,128)(2,1)}) custom-call(bf16[256,2048]{1,0:T(8,128)(2,1)} %refs_1_.3, bf16[1,1024,2048]{2,1,0:T(8,128)(2,1)} %refs_2_.1, f32[1,2048]{1,0:T(1,128)} %get-tuple-element.38.refs_2_, ...), custom_call_target="tpu_custom_call" | custom-call | flops 30000001024 | bytes 30000000 | tf_op jit(solution)/shard_map/attention0/pallas_call | solution.py:389
  104.5 105.0 %mlp0.1 = (bf16[5,64,2048]{2,1,0:T(8,128)(2,1)}, bf16[5,64,2048]{2,1,0:T(8,128)(2,1)}) custom-call(bf16[5,64,2048]{2,1,0:T(8,128)(2,1)} %get-tuple-element.13.refs_0_, bf16[256,2048]{1,0:T(8,128)(2,1)} %refs_1_.3, bf16[1,1024,2048]{2,1,0:T(8,128)(2,1)} %refs_2_.1, f32[1,2048]{1,0:T(1,128)} %get-tuple-element.28.refs_3_, ...), custom_call_target="tpu_custom_call" | custom-call | flops 80000000000 | bytes 80000000 | tf_op jit(solution)/shard_map/mlp0/pallas_call | solution.py:532
  209.5 0.0 copy-start
  209.5 5.1 %copy_bitcast_fusion = (bf16[2048,512]{1,0:T(8,128)(2,1)}, bf16[2048,512]{1,0:T(8,128)(2,1)}) fusion(bf16[256,8,4,128]{3,2,1,0:T(4,128)(2,1)} %bitcast.33, bf16[256,8,4,128]{3,2,1,0:T(4,128)(2,1)} %bitcast.34), kind=kLoop, calls=%fused_computation | loop fusion | bytes 8388608 | tf_op jit(solution)/shard_map/reshape;squeeze | solution.py:675
  214.6 0.0 copy-done
  214.6 1.8 copy.28
  216.4 112.0 %attention1.1 = (bf16[4,64,2048]{2,1,0:T(8,128)(2,1)}, bf16[4,512,2048]{2,1,0:T(8,128)(2,1)}, bf16[4,512,256]{2,1,0:T(8,128)(2,1)}, bf16[4,1376,256]{2,1,0:T(8,128)(2,1)}) custom-call(bf16[5,64,2048]{2,1,0:T(8,128)(2,1)} %get-tuple-element.16.refs_0_, bf16[2048,512]{1,0:T(8,128)(2,1)} %bitcast.37, bf16[2048,512]{1,0:T(8,128)(2,1)} %get-tuple-element.41.refs_2_, ...), custom_call_target="tpu_custom_call" | custom-call | flops 30000001024 | bytes 30000000 | tf_op jit(solution)/shard_map/attention1/pallas_call | solution.py:389
  328.4 88.2 %mlp1.1.h_in = bf16[4,64,2048]{2,1,0:T(8,128)(2,1)} custom-call(bf16[4,64,2048]{2,1,0:T(8,128)(2,1)} %get-tuple-element.17.refs_0_, bf16[5,64,2048]{2,1,0:T(8,128)(2,1)} %get-tuple-element.18.refs_1_, f32[1,2048]{1,0:T(1,128)} %get-tuple-element.27.refs_2_, f32[1,2048]{1,0:T(1,128)} %bitcast.48, bf16[2,512,2048]{2,1,0:T(8,128)(2,1)} %bitcast.47, ...), custom_call_target="tpu_custom_call" | custom-call | flops 80000000000 | bytes 80000000 | tf_op jit(solution)/shard_map/mlp1/pallas_call | solution.py:532
  416.6 1.7 broadcast_in_dim.14.target
  419.0 74.0 %head.1 = f32[1,1024]{1,0:T(1,128)} custom-call(bf16[4,64,2048]{2,1,0:T(8,128)(2,1)} %mlp1.1.h_in, bf16[2048,8192]{1,0:T(8,128)(2,1)} %wv.1, s32[1024,128]{1,0:T(8,128)} %broadcast_in_dim.14.target, s32[1]{0:T(128)S(6)} %copy.31.lens), custom_call_target="tpu_custom_call" | custom-call | flops 40000000000 | bytes 40000000 | tf_op jit(solution)/shard_map/head/pallas_call | solution.py:634
  492.9 1.3 copy.32
  (4 shorter events, 0.0 us)
Async XLA Ops:
  0.0 3.9 copy-start.1
  3.9 2.9 copy-start.2
  9.3 2.8 copy-start.4
  9.3 2.8 copy-start.5
  9.3 3.5 copy-start.3
  209.5 5.1 %copy-start = (bf16[1,2048,4,128]{3,2,1,0:T(4,128)(2,1)S(1)}, bf16[1,2048,4,128]{3,2,1,0:T(4,128)(2,1)}, u32[]{:S(2)}) copy-start(bf16[1,2048,4,128]{3,2,1,0:T(4,128)(2,1)} %get-tuple-element.25) | copy-start | bytes 6291460

commit v3 on v2

v3 whole, which is shorter than its diff:
```python
import functools

import jax
import jax.numpy as jnp
from jax import lax
from jax.experimental import pallas as pl
from jax.experimental.pallas import tpu as pltpu
from jax.sharding import PartitionSpec as P

EPS = 1e-6
ROPE_BASE = 10000.0
LOG2E = 1.4426950408889634
VMEM_BYTES = 67043328
ROWS = 64
LANES = 128
BLOCK = 256
BF = jnp.bfloat16
F32 = jnp.float32
ANY = pl.BlockSpec(memory_space=pl.ANY)
VM = pl.BlockSpec(memory_space=pltpu.VMEM)
MESH = pl.DeviceIdType.MESH
RIGHT, LEFT, RIGHT_ON, LEFT_ON, OWN_MATE, LEFT_MATE, RIGHT_MATE, OPP_MATE = range(8)


def ds(index, size):
    return pl.ds(pl.multiple_of(index * size, size), size)


def dot(a, b):
    return jnp.dot(a, b, preferred_element_type=F32)


def dot_t(a, b):
    return lax.dot_general(a, b, (((1,), (1,)), ((), ())), preferred_element_type=F32)


def sems(*shape):
    return pltpu.SemaphoreType.DMA(shape)


def remote(src, dst, send, recv, axis, where):
    return pltpu.make_async_remote_copy(src_ref=src, dst_ref=dst, send_sem=send, recv_sem=recv, device_id={axis: where}, device_id_type=MESH)


def local(src, dst, sem):
    copy = pltpu.make_async_copy(src, dst, sem)
    copy.start()
    return copy


def greet(rings):
    barrier = pltpu.get_barrier_semaphore()
    peers = {}
    for ring in rings:
        for i, where in enumerate(ring.places[1:]):
            peers[ring.axis, i] = (ring.axis, where)
        if ring.mate is not None:
            peers['mate'] = (ring.axis, ring.mate)
    for axis, where in peers.values():
        pl.semaphore_signal(barrier, inc=1, device_id={axis: where}, device_id_type=MESH)
    pl.semaphore_wait(barrier, len(peers))


class Ring:
    def __init__(self, axis, me, stride, piece, send, recv, source=None, mate=None):
        self.axis, self.piece, self.send, self.recv, self.source, self.mate = axis, piece, send, recv, source, mate
        self.places = [lax.rem(me + k * stride, 4 * stride) for k in range(4)]
        self.own, self.right, self.opp, self.left = self.places
        self.mate_step = None if mate is None else mate - me

    def copy(self, kind, u, owner, source=None):
        dst = self.piece(u, owner)
        if kind in (RIGHT_ON, LEFT_ON):
            half = dst.shape[0] // 2
            dst = dst.at[pl.ds((kind - RIGHT_ON) * half, half)]
        where = self.mate if kind >= OWN_MATE else self.left if kind in (LEFT, LEFT_ON) else self.right
        return remote(dst if source is None else source, dst, self.send.at[kind, u], self.recv.at[kind, u], self.axis, where)

    def start(self, u):
        for kind in (OWN_MATE, RIGHT, LEFT)[self.mate is None:]:
            self.copy(kind, u, self.own, self.source and self.source(u)).start()

    def forward(self, u):
        for kind, owner in ((RIGHT, self.left), (LEFT, self.right)):
            self.copy(kind, u, owner).wait_recv()
            self.copy(kind + RIGHT_ON, u, owner).start()
            if self.mate is not None:
                self.copy(kind + LEFT_MATE, u, owner).start()

    def finish(self, u):
        for kind in (RIGHT_ON, LEFT_ON):
            self.copy(kind, u, self.opp).wait_recv()
        if self.mate is not None:
            self.copy(OPP_MATE, u, self.opp).start()

    def mate_has(self, u, kind):
        owner = {OWN_MATE: self.own, LEFT_MATE: self.left, RIGHT_MATE: self.right, OPP_MATE: self.opp}[kind]
        self.copy(kind, u, owner + self.mate_step).wait_recv()

    def mate_arrived(self, u):
        for kind in range(OWN_MATE, OPP_MATE + 1):
            self.mate_has(u, kind)

    def drain(self, u):
        for kind, owner in ((RIGHT, self.own), (LEFT, self.own), (RIGHT_ON, self.left), (LEFT_ON, self.right), (OWN_MATE, self.own), (LEFT_MATE, self.left), (RIGHT_MATE, self.right), (OPP_MATE, self.opp)):
            if kind < OWN_MATE or self.mate is not None:
                self.copy(kind, u, owner).wait_send()


def resp_ring(piece, send, recv, source=None):
    r = lax.axis_index('resp')
    return Ring('resp', r, 2, piece, send, recv, source, r + 1 - 2 * lax.rem(r, 2))


def model_ring(piece, send, recv, source=None):
    return Ring('model', lax.axis_index('model'), 1, piece, send, recv, source)


def norm_rows(src, dst, gain_ref, rows, width):
    def square(n, total):
        block = src(ds(n, BLOCK)).astype(F32)
        sq = block * block
        return total + sq[:, :LANES] + sq[:, LANES:]

    trips = width // BLOCK
    total = lax.fori_loop(0, trips, square, jnp.zeros((rows, LANES), F32), unroll=2)
    inv = lax.rsqrt(jnp.sum(total, axis=-1, keepdims=True) / width + EPS)

    def scale(n, carry):
        cols = ds(n, BLOCK)
        dst(cols, (src(cols).astype(F32) * inv * gain_ref[:, cols]).astype(BF))
        return carry

    lax.fori_loop(0, trips, scale, 0, unroll=2)


def loop(lo, hi, body):
    def wrapped(i, carry):
        body(i)
        return carry
    lax.fori_loop(lo, hi, wrapped, 0)


def when(condition, *actions):
    @pl.when(condition)
    def _():
        for action in actions:
            action()


def params(collective):
    return pltpu.CompilerParams(collective_id=collective, has_side_effects=True, vmem_limit_bytes=VMEM_BYTES)


def work(flops):
    return pl.CostEstimate(flops=flops, bytes_accessed=flops // 1000, transcendentals=0)


def attention_kernel(first, layer, chunks, *refs):
    if first:
        xp, xr, gain, *refs = refs
    else:
        h0, hin, *refs = refs
    cos, sin, *refs = refs
    heads_in, (w_out, w_down, o_out, wo_all, wd_y, *refs) = refs[:3], refs[3:]
    if first:
        wo_y, wo_next, x_v, *refs = refs
    else:
        wo_y = w_out
    raw_v, w_v, raw_s, h_v, q_v, k_v, v_v, acc_v, m_v, l_v, o_v, load, h_s, h_r, kv_s, kv_r, y_s, y_r, wo_s, wo_r, o_s, o_r, own_s = refs
    me, r = lax.axis_index('model'), lax.axis_index('resp')
    chip = r // 2
    _, dim, width = w_v.shape
    heads = width // LANES
    log_scale = LOG2E * LANES ** -0.5
    prompt_blocks = k_v.shape[0] - (chunks - 1)

    gather = model_ring(lambda c, b: h_v.at[c, b], h_s, h_r)
    kv = resp_ring(lambda u, b: (k_v, v_v)[u].at[b], kv_s, kv_r)
    ours = ds(r, BLOCK)
    spread = model_ring(lambda u, b: (wd_y, wo_y, wo_next if first else None)[u].at[b], y_s, y_r, lambda u: (w_down, w_out, w_out)[u].at[layer + u // 2, :, ours])
    shares = spread.places[1:]
    outs = resp_ring(lambda u, b: wo_all.at[shares[u], :, ds(b, BLOCK)], wo_s, wo_r, lambda u: wo_y.at[shares[u]])

    raws = [local(w.at[layer], raw_v.at[i], raw_s.at[i]) for i, w in enumerate(heads_in)]

    def x_load(c):
        return pltpu.make_async_copy(xr.at[0, ds(c - 1, BLOCK)], x_v.at[c], load.at[c])

    if first:
        loads = [local(xp, x_v.at[0], load.at[0])]
        for c in range(1, chunks):
            x_load(c).start()
    else:
        loads = [local(h0, h_v.at[0], load.at[0])] + [local(hin.at[c], h_v.at[c, me], load.at[c]) for c in range(1, chunks)]
    greet([gather, kv])

    def own_cols(s):
        return pltpu.make_async_copy(wo_y.at[shares[s]], wo_all.at[shares[s], :, ours], own_s.at[s])

    def start_whole_out():
        for s in range(3):
            outs.start(s)
            own_cols(s).start()

    def key_block(c):
        return jnp.where(c == 0, r, prompt_blocks + c - 1)

    def flatten():
        for i, raw in enumerate(raws):
            raw.wait()

            def part(n):
                w_v[i, ds(n, BLOCK)] = raw_v[i, ds(n, BLOCK)].reshape(BLOCK, width)
            loop(0, dim // BLOCK, part)

    def project(c, then=None):
        rows = pl.ds(pl.multiple_of(c * BLOCK, BLOCK), BLOCK)
        cs, sn = cos[rows, :], sin[rows, :]
        blk = key_block(c)
        for which in range(3):
            if which == 2 and then is not None:
                then()
            for n in range(width // BLOCK):
                y = dot(h_v[c].reshape(BLOCK, dim), w_v[which, :, pl.ds(n * BLOCK, BLOCK)])
                for i in range(2):
                    cols = pl.ds((2 * n + i) * LANES, LANES)
                    part = y[:, i * LANES:(i + 1) * LANES]
                    if which == 1:
                        v_v[blk, cols, :] = part.T.astype(BF)
                    else:
                        part = (part * cs + pltpu.roll(part, LANES // 2, 1) * sn).astype(BF)
                        if which == 2:
                            q_v[c, :, cols] = part
                        else:
                            k_v[blk, :, cols] = part

    def kv_do(*names):
        for name in names:
            for u in range(2):
                getattr(kv, name)(u)

    key_i = lax.broadcasted_iota(jnp.int32, (BLOCK, BLOCK), 0)
    causal = key_i <= lax.broadcasted_iota(jnp.int32, (BLOCK, BLOCK), 1)

    def step(qi, kb, blocks, diagonal=False):
        def scores(n):
            cols = pl.ds(n * LANES, LANES)
            s = dot_t(k_v[pl.ds(kb, blocks), :, cols].reshape(blocks * BLOCK, LANES), q_v[qi, :, cols])
            return jnp.where(causal, s, -jnp.inf) if diagonal else s

        kept = [scores(n) for n in range(heads)]
        tops = [jnp.max(s, axis=0, keepdims=True) for s in kept]
        for n in range(heads):
            s, top = kept[n], tops[n]
            if not diagonal:
                m = m_v[qi, n, :1]
                top = jnp.maximum(m, top)
            p = jnp.exp2((s - top) * log_scale)
            total = jnp.sum(p, axis=0, keepdims=True)
            p = p.astype(BF)
            mixed = None
            for b in range(blocks):
                part = dot(v_v[kb + b, pl.ds(n * LANES, LANES), :], p[b * BLOCK:(b + 1) * BLOCK])
                mixed = part if mixed is None else mixed + part
            if not diagonal:
                alpha = jnp.exp2((m - top) * log_scale)
                total = total + l_v[qi, n, :1] * alpha
                mixed = mixed + acc_v[qi, n] * alpha
            m_v[qi, n, :1] = top
            l_v[qi, n, :1] = total
            acc_v[qi, n] = mixed

    low = 0 if first else 1

    def own(qi):
        step(qi, key_block(qi), 1, True)
        loop(prompt_blocks, prompt_blocks + qi - 1, lambda b: step(qi, b, 1))

    def o_copy(c, k):
        owner = spread.places[k]
        return remote(o_v.at[c, owner], o_out.at[c, :, ds(me, width)], o_s.at[k - 1, c], o_r.at[k - 1, c], 'model', owner)

    def o_own(c):
        return pltpu.make_async_copy(o_v.at[c, me], o_out.at[c, :, ds(me, width)], load.at[c])

    def own_chip(qi):
        when(qi > 0, lambda: step(qi, 2 * chip, 2))
        when((qi == 0) & (r > 2 * chip), lambda: step(qi, 2 * chip, 1))

    def prompt(qi):
        c = qi - low
        if first:
            loop(jnp.where(qi == 0, 4 - chip, 1), 4, lambda x: step(qi, 2 * lax.rem(chip + x, 4), 2))
        else:
            loop(jnp.where(qi == 0, 4, 0), 4, lambda x: step(qi, 2 * x, 2))
        for n in range(heads):
            out = (acc_v[qi, n] / l_v[qi, n, :1]).T.astype(BF)
            o_v[c, :, :, pl.ds(n * LANES, LANES)] = out.reshape(4, ROWS, LANES)
        for k in (2, 1, 3):
            o_copy(c, k).start()
        o_own(c).start()

    def whole_out(*names):
        for name in names:
            for u in range(3):
                getattr(outs, name)(u)

    if first:
        spread.start(1)
        flatten()

        def chunk(c):
            when(c > 0, lambda: x_load(c).wait())
            norm_rows(lambda cols: x_v[c, :, cols], lambda cols, val: h_v.__setitem__((c, slice(None), slice(None), cols), val.reshape(4, ROWS, BLOCK)), gain, BLOCK, dim)
            project(c, lambda: when(c == 0, lambda: kv_do('start')))
            when(c == 1, lambda: (spread.forward(1), spread.start(0)))

        loads[0].wait()
        loop(0, chunks, chunk)

        def own_and_pass(qi):
            own(qi)

            def pass_on():
                kv_do('forward')
                spread.finish(1)
                start_whole_out()
            when(qi == 1, pass_on)

        loop(low, chunks, own_and_pass)
        for u in range(2):
            kv.mate_has(u, OWN_MATE)
        loop(low, chunks, own_chip)
        kv_do('finish')
        spread.forward(0)
        spread.start(2)
        for u in range(2):
            for kind in (LEFT_MATE, RIGHT_MATE, OPP_MATE):
                kv.mate_has(u, kind)

        def prompt_and_events(qi):
            prompt(qi)
            when(qi == 3, lambda: (whole_out('forward'), spread.forward(2)))

        loop(low, chunks, prompt_and_events)
    else:
        for cp in loads:
            cp.wait()
        for c in (1, 2):
            gather.start(c)
        flatten()
        project(jnp.int32(0))
        kv_do('start')

        def chunk(c):
            def receive():
                gather.forward(c)
                when(c + 2 < chunks, lambda: gather.start(c + 2))
            when(c < chunks, receive)
            when(c == 3, lambda: kv_do('finish', 'mate_arrived'))
            when(c == 4, lambda: spread.start(0))
            when(c == 5, lambda: whole_out('forward'))
            when(c >= 3, lambda: prompt(c - 2))

            def use():
                gather.finish(c - 1)
                project(c - 1)
                own(c - 1)
            when((c > 1) & (c <= chunks), use)
            when(c == 2, lambda: (kv_do('forward'), start_whole_out()))
            when(c == 5, lambda: spread.forward(0))

        loop(1, chunks + 2, chunk)
    whole_out('finish')
    spread.finish(0)
    if first:
        spread.finish(2)
    for s in range(3):
        outs.mate_arrived(s)
        outs.drain(s)
        own_cols(s).wait()
    for u in range(2):
        kv.drain(u)
    for u in range(3 if first else 1):
        spread.drain(u)
    for c in range(chunks - low):
        for k in (1, 2, 3):
            o_copy(c, k).wait()
        o_own(c).wait()
    if not first:
        for c in range(1, chunks):
            gather.drain(c)


def attention(first, layer, collective, hidden, gain, cos, sin, heads_in, w_out, w_down):
    _, dim, *by_head = heads_in[0].shape
    width = by_head[0] * by_head[1]
    chunks = cos.shape[0] // BLOCK
    outs = chunks if first else chunks - 1
    heads = width // LANES
    blocks = lax.psum(1, 'resp') + chunks - 1
    tables = ((gain,) if first else ()) + (cos, sin)
    args = (*hidden, *tables, *heads_in, w_out, w_down)
    specs = [ANY] * len(hidden) + [VM] * len(tables) + [ANY] * 5
    ffn = w_down.shape[1]
    shapes = [(outs, ROWS, 4 * width), (4, width, dim), (4, ffn, BLOCK)] + ([(4, width, BLOCK)] * 2 if first else [])
    scratch = [pltpu.VMEM((chunks, BLOCK, dim), BF)] if first else []
    state = pltpu.VMEM((chunks, heads, 8, BLOCK), F32)
    scratch += [
        pltpu.VMEM((3, dim, *by_head), BF),
        pltpu.VMEM((3, dim, width), BF),
        sems(3),
        pltpu.VMEM((chunks, 4, ROWS, dim), BF),
        pltpu.VMEM((chunks, BLOCK, width), BF),
        pltpu.VMEM((blocks, BLOCK, width), BF),
        pltpu.VMEM((blocks, width, BLOCK), BF),
        pltpu.VMEM((chunks, heads, LANES, BLOCK), F32),
        state,
        state,
        pltpu.VMEM((outs, 4, ROWS, width), BF),
        sems(chunks),
    ]
    for kinds, units in ((4, chunks), (8, 2), (4, 3), (8, 3), (3, outs)):
        scratch += [sems(kinds, units)] * 2
    scratch.append(sems(3))
    return pl.pallas_call(
        functools.partial(attention_kernel, first, layer, chunks),
        name=f'attention{layer}',
        out_shape=tuple(jax.ShapeDtypeStruct(s, BF) for s in shapes),
        in_specs=specs,
        out_specs=(ANY,) * len(shapes),
        scratch_shapes=scratch,
        compiler_params=params(collective),
        cost_estimate=work(30_000_000_000),
    )(*args)


def mlp_kernel(first, layer, chunks, *refs):
    o_in, *refs = refs
    count = 2 if first else 1
    rows_in, (gain, next_gain, w_out, wo_all, wg, wu, w_down, wd_y, h_out, h0_out, *refs) = refs[:count], refs[count:]
    if first:
        x_out, *refs = refs
    wo_v, wg_v, wu_v, wd_v, o_v, x_v, u_v, si_v, ri_v, acc_v, hg_v, load, wl, wd_l, wo_l, g_s, g_r, h_s, h_r, x_s, x_r, i_s, i_r = refs
    me, r = lax.axis_index('model'), lax.axis_index('resp')
    dim = x_v.shape[-1]
    ffn = wg_v.shape[0]
    width = wo_v.shape[1]
    rows = chunks * ROWS
    gather = model_ring(lambda c, b: u_v.at[c, b], h_s, h_r)
    shares = gather.places[1:]
    downs = resp_ring(lambda u, b: wd_v.at[u + 1, :, ds(b, BLOCK)], x_s, x_r, lambda u: wd_y.at[shares[u]])
    ahead = model_ring(lambda u, b: hg_v.at[b], g_s, g_r)

    def wo_load(n):
        cols = ds(n, 2 * BLOCK)
        sources = [w_out.at[layer]] + [wo_all.at[s] for s in shares]
        return [pltpu.make_async_copy(src.at[:, cols], wo_v.at[s, :, cols], wo_l.at[i, n]) for i, (s, src) in enumerate(zip(gather.places, sources))]

    start = [local(o_in, o_v, load.at[0])]
    column_loads = dim // (2 * BLOCK)
    loop(0, column_loads, lambda n: [cp.start() for cp in wo_load(n)])
    if first:
        start += [local(rows_in[0].at[ds(me, ROWS)], x_v.at[0], load.at[1])]
        start += [local(rows_in[1].at[0, ds((c - 1) * 4 + me, ROWS)], x_v.at[c], load.at[1 + c]) for c in range(1, chunks)]
    else:
        start += [local(rows_in[0].at[pl.ds(1, chunks)], x_v, load.at[1])]
    greet([gather, downs])
    downs.start(2)
    downs.start(1)
    for cp in start:
        cp.wait()

    def outproj(n):
        cols = ds(n, 2 * BLOCK)
        for cp in wo_load(n):
            cp.wait()
        y = dot(o_v[...].reshape(rows, dim), wo_v[:, :, cols].reshape(dim, 2 * BLOCK))
        x_v[:, :, cols] = (x_v[:, :, cols].reshape(rows, 2 * BLOCK).astype(F32) + y).astype(BF).reshape(chunks, ROWS, 2 * BLOCK)

    loop(0, column_loads, outproj)
    weights = [local(wg.at[layer], wg_v, wl.at[4]), local(wu.at[layer], wu_v, wl.at[5])]
    kept = [local(w_down.at[layer], wd_v.at[0], wd_l.at[0])]
    kept += [local(wd_y.at[s], wd_v.at[i, :, ds(r, BLOCK)], wd_l.at[i]) for i, s in enumerate(shares, 1)]

    def normalize(c):
        norm_rows(lambda cols: x_v[c, :, cols], lambda cols, val: u_v.__setitem__((c, me, slice(None), cols), val), gain, ROWS, dim)
        when(c < 2, lambda: gather.start(c))

    loop(0, chunks, normalize)
    for cp in weights:
        cp.wait()

    def i_send(c, k):
        return remote(si_v.at[c, gather.places[k]], ri_v.at[4 - k, c], i_s.at[k - 1, c], i_r.at[k - 1, c], 'model', gather.places[k])

    def i_recv(c, q):
        ref = ri_v.at[q, c]
        return remote(ref, ref, i_s.at[3 - q, c], i_r.at[3 - q, c], 'model', lax.rem(me + q, 4))

    def gate_up(c):
        lhs = u_v[c].reshape(4 * ROWS, dim)
        half = ffn // 2
        for lo in (0, half):
            cols = pl.ds(lo, half)
            g = dot_t(lhs, wg_v[cols, :])
            inner = (g * jax.nn.sigmoid(g) * dot_t(lhs, wu_v[cols, :])).astype(BF)
            si_v[c, :, :, cols] = inner.reshape(4, ROWS, half)
        for k in (1, 2, 3):
            i_send(c, k).start()
        ri_v[0, c] = si_v[c, me]

    events = {1: lambda: (downs.forward(2), downs.start(0)), 3: lambda: (downs.forward(1), downs.finish(2))}

    def chunk(c):
        def receive():
            gather.forward(c)
            when(c + 2 < chunks, lambda: gather.start(c + 2))
        when(c < chunks, receive)

        def use():
            gather.finish(c - 1)
            gate_up(c - 1)
        when(c > 0, use)
        for at, event in events.items():
            when(c == at, event)

    loop(0, chunks + 1, chunk)
    downs.forward(0)
    downs.finish(1)
    for cp in kept:
        cp.wait()

    def down(lo, hi):
        size = hi - lo
        head = lo == 0
        shape = (size, ROWS, 2 * BLOCK)
        flat = pl.ds(0, size * ROWS)

        def load_rows(n):
            cols = ds(n, 2 * BLOCK)
            acc_v[flat, cols] = x_v[lo:hi, :, cols].reshape(size * ROWS, 2 * BLOCK).astype(F32)

        def store_rows(n):
            cols = ds(n, 2 * BLOCK)
            x_v[lo:hi, :, cols] = acc_v[flat, cols].astype(BF).reshape(shape)

        def product(i):
            q = lax.rem(4 - i, 4)

            def arrive():
                for c in range(lo, hi):
                    i_recv(c, q).wait_recv()
                if head:
                    downs.mate_arrived(q - 1)
            if head:
                when(i == 3, lambda: downs.finish(0))
            else:
                when(i == 2, lambda: ahead.forward(0))
            when(i > 0, arrive)

            def tile(n):
                cols = ds(n, 4 * BLOCK)
                acc_v[flat, cols] = acc_v[flat, cols] + dot(ri_v[q, lo:hi].reshape(size * ROWS, ffn), wd_v[q, :, cols])

            loop(0, dim // (4 * BLOCK), tile)

        loop(0, dim // (2 * BLOCK), load_rows)
        loop(0, 4, product)
        loop(0, dim // (2 * BLOCK), store_rows)
        norm_rows(lambda cols: x_v[lo:hi, :, cols].reshape(size * ROWS, BLOCK), lambda cols, val: o_v.__setitem__((slice(lo, hi), slice(None), cols), val.reshape(size, ROWS, BLOCK)), next_gain, size * ROWS, dim)
        if head:
            hg_v[me] = o_v[0]
            ahead.start(0)
        else:
            ahead.finish(0)

    split = (chunks + 1) // 2
    stored = []
    for part, (lo, hi) in enumerate(((0, split), (split, chunks))):
        down(lo, hi)
        span = pl.ds(lo, hi - lo)
        stored.append(local(o_v.at[span], h_out.at[span], load.at[part]))
        if first:
            stored.append(local(x_v.at[span], x_out.at[span], load.at[2 + part]))
    stored.append(local(hg_v, h0_out, load.at[4]))
    for cp in stored:
        cp.wait()
    ahead.drain(0)
    for u in range(3):
        downs.drain(u)
    for c in range(chunks):
        gather.drain(c)
        for k in (1, 2, 3):
            i_send(c, k).wait_send()


def mlp(first, layer, collective, o_in, rows_in, gain, next_gain, w_out, wo_all, wg, wu, w_down, wd_y):
    chunks, _, dim = o_in.shape
    ffn = wg.shape[1]
    args = (o_in, *rows_in, gain, next_gain, w_out, wo_all, wg, wu, w_down, wd_y)
    specs = [ANY] * (1 + len(rows_in)) + [VM] * 2 + [ANY] * 6
    rows = (chunks, ROWS, dim)
    shapes = [rows, (4, ROWS, dim)] + ([rows] if first else [])
    scratch = [pltpu.VMEM(s, BF) for s in (wo_all.shape, (ffn, dim), (ffn, dim), (4, ffn, dim), (chunks, ROWS, dim), (chunks, ROWS, dim), (chunks, 4, ROWS, dim), (chunks, 4, ROWS, ffn), (4, chunks, ROWS, ffn))]
    scratch += [pltpu.VMEM(((chunks + 1) // 2 * ROWS, dim), F32), pltpu.VMEM((4, ROWS, dim), BF), sems(6), sems(6), sems(4), sems(4, 4)]
    for kinds, units in ((4, 1), (4, chunks), (8, 3), (3, chunks)):
        scratch += [sems(kinds, units)] * 2
    return pl.pallas_call(
        functools.partial(mlp_kernel, first, layer, chunks),
        name=f'mlp{layer}',
        out_shape=tuple(jax.ShapeDtypeStruct(s, BF) for s in shapes),
        in_specs=specs,
        out_specs=(ANY,) * len(shapes),
        scratch_shapes=scratch,
        compiler_params=params(collective),
        cost_estimate=work(80_000_000_000),
    )(*args)


def head_kernel(chunks, tiles, h0, h_in, wv, target, lens, out, wv_v, u_v, even_v, odd_v, m_v, l_v, p_v, t_v, st_v, load, wl, h_s, h_r, st_s, st_r):
    me = lax.axis_index('model')
    dim, vocab = wv_v.shape
    span = vocab // tiles
    tile = 4 * BLOCK
    gather = model_ring(lambda c, b: u_v.at[c, b], h_s, h_r)
    rows = [local(h0, u_v.at[0], load.at[0])] + [local(h_in.at[c], u_v.at[c, me], load.at[c]) for c in range(1, chunks)]

    def weight(t):
        cols = ds(t, span)
        return pltpu.make_async_copy(wv.at[:, cols], wv_v.at[:, cols], wl.at[t])

    weight(0).start()
    greet([gather])
    for cp in rows:
        cp.wait()
    for c in (1, 2):
        gather.start(c)
    lane = lax.broadcasted_iota(jnp.int32, (BLOCK, LANES), 1)
    pieces = range(tile // LANES)
    count = vocab // tile
    per = span // tile

    def logits(c, n):
        return dot(u_v[c].reshape(BLOCK, dim), wv_v[:, ds(n, tile)])

    def reduce_tile(s_v, n):
        parts = [s_v[:, i * LANES:(i + 1) * LANES] for i in pieces]
        m = m_v[...]
        top = functools.reduce(jnp.maximum, parts, m)
        total = l_v[...] * jnp.exp2((m - top) * LOG2E)
        picked = p_v[...]
        wanted = t_v[...] - n * tile
        for i in pieces:
            total = total + jnp.exp2((parts[i] - top) * LOG2E)
            picked = picked + jnp.where(wanted - i * LANES == lane, parts[i], 0.0)
        m_v[...] = top
        l_v[...] = total
        p_v[...] = picked

    def vocab_pass(c):
        m_v[...] = jnp.full_like(m_v, -jnp.inf)
        l_v[...] = jnp.zeros_like(l_v)
        p_v[...] = jnp.zeros_like(p_v)
        t_v[...] = jnp.broadcast_to(target[:, ds(c, BLOCK)], (LANES, BLOCK)).T - me * vocab
        when(c == 0, lambda: (weight(0).wait(), weight(1).start()))
        even_v[...] = logits(c, 0)

        def columns(i):
            n = 2 * i

            def next_weight():
                t = (n + 2) // per
                weight(t).wait()
                when(t + 1 < tiles, lambda: weight(t + 1).start())
            when((c == 0) & (lax.rem(n + 2, per) == 0), next_weight)
            when((i == 1) & (c + 1 < chunks), lambda: pass_on(c + 1))
            odd_v[...] = logits(c, n + 1)
            reduce_tile(even_v, n)
            even_v[...] = logits(c, n + 2)
            reduce_tile(odd_v, n + 1)

        loop(0, count // 2 - 1, columns)
        odd_v[...] = logits(c, count - 1)
        reduce_tile(even_v, count - 2)
        reduce_tile(odd_v, count - 1)
        m = m_v[...]
        top = jnp.max(m, axis=-1, keepdims=True)
        total = jnp.sum(l_v[...] * jnp.exp2((m - top) * LOG2E), axis=-1, keepdims=True)
        picked = jnp.sum(p_v[...], axis=-1, keepdims=True)
        stat = jnp.where(lane == 0, top, jnp.where(lane == 1, total, picked))
        st_v[me, :, ds(c, BLOCK)] = stat.T[:8]

    def pass_on(c):
        gather.forward(c)
        when(c + 2 < chunks, lambda: gather.start(c + 2))

    def chunk(c):
        when(c > 0, lambda: gather.finish(c))
        vocab_pass(c)

    loop(0, chunks, chunk)

    def st_copy(k, block):
        return remote(st_v.at[block], st_v.at[block], st_s.at[k - 1], st_r.at[k - 1], 'model', gather.places[k])

    for k in (2, 1, 3):
        st_copy(k, me).start()
    for k in (1, 2, 3):
        st_copy(k, gather.places[4 - k]).wait_recv()
    tops = [st_v[s, 0:1, :] for s in range(4)]
    top = functools.reduce(jnp.maximum, tops)
    total = sum(st_v[s, 1:2, :] * jnp.exp2((tops[s] - top) * LOG2E) for s in range(4))
    value = sum(st_v[s, 2:3, :] for s in range(4)) - top - jnp.log(total)
    token = lax.broadcasted_iota(jnp.int32, value.shape, 1)
    out[...] = jnp.where(token < lens[0], value, 0.0)
    for k in (1, 2, 3):
        st_copy(k, me).wait_send()
    for c in range(1, chunks):
        gather.drain(c)


def head(collective, h0, h_in, wv, target, lens):
    chunks, _, dim = h_in.shape
    tiles = 4
    stat = pltpu.VMEM((BLOCK, LANES), F32)
    scores = pltpu.VMEM((BLOCK, 4 * BLOCK), F32)
    return pl.pallas_call(
        functools.partial(head_kernel, chunks, tiles),
        name='head',
        out_shape=jax.ShapeDtypeStruct((1, chunks * BLOCK), F32),
        in_specs=[ANY, ANY, ANY, VM, pl.BlockSpec(memory_space=pltpu.SMEM)],
        out_specs=VM,
        scratch_shapes=[
            pltpu.VMEM(wv.shape, BF),
            pltpu.VMEM((chunks, 4, ROWS, dim), BF),
            scores,
            scores,
            stat,
            stat,
            stat,
            pltpu.VMEM((BLOCK, LANES), jnp.int32),
            pltpu.VMEM((4, 8, chunks * BLOCK), F32),
            sems(chunks),
            sems(tiles),
        ] + [sems(4, chunks)] * 2 + [sems(3)] * 2,
        compiler_params=params(collective),
        cost_estimate=work(40_000_000_000),
    )(h0, h_in, wv, target, lens)


def rope_tables(prompt_rows, resp_len, groups):
    half = LANES // 2
    freq = ROPE_BASE ** (-jnp.arange(half, dtype=F32) / half)
    pos = jnp.concatenate([lax.axis_index('resp') * prompt_rows + jnp.arange(prompt_rows), prompt_rows * groups + jnp.arange(resp_len)])
    angles = pos.astype(F32)[:, None] * freq
    c, s = jnp.cos(angles), jnp.sin(angles)
    return jnp.concatenate([c, c], axis=-1), jnp.concatenate([-s, s], axis=-1)


def solution(mesh):
    groups = mesh.shape['resp']
    row_axes = ('prompts', 'resp')
    head_spec = P(None, None, 'model', None)
    in_specs = (P(row_axes, None), P(row_axes, None, None), P(row_axes, None), P(row_axes), P(None, None), head_spec, head_spec, head_spec, P(None, 'model', None, None), P(None, None), P(None, None, 'model'), P(None, None, 'model'), P(None, 'model', None), P(None), P(None, 'model'))

    def device_step(x_prompt, x_resp, targets, resp_lens, attn_gain, w_query, w_key, w_value, w_out, mlp_gain, w_gate, w_up, w_down, final_gain, w_vocab):
        layers, dim, heads, head_dim = w_query.shape
        width = heads * head_dim
        resp_len = x_resp.shape[1]
        cos, sin = rope_tables(x_prompt.shape[0], resp_len, groups)
        w_out = w_out.reshape(layers, width, dim)
        gates = [jnp.swapaxes(w, 1, 2) for w in (w_gate, w_up)]
        gains = [attn_gain[l:l + 1] for l in range(layers)] + [final_gain[None, :]]
        rows = (x_prompt, x_resp)
        hidden = rows
        wo_y = w_out
        for l in range(layers):
            first = l == 0
            o, wo_all, wd_y, *spread = attention(first, l, 2 * l, hidden, gains[l], cos, sin, (w_key, w_value, w_query), wo_y, w_down)
            h, h0, *rows = mlp(first, l, 2 * l + 1, o, rows, mlp_gain[l:l + 1], gains[l + 1], w_out, wo_all, *gates, w_down, wd_y)
            if first:
                wo_y = spread[1]
            hidden = (h0, h)
        return head(2 * layers, h0, h, w_vocab, targets, resp_lens)

    return jax.shard_map(device_step, mesh=mesh, in_specs=in_specs, out_specs=P(row_axes, None), check_vma=False)
```

time: 495 us -> 414 us (0.84)
  Pallas kernels: 467 us -> 407 us
  local copies, waits for them, and re-layouts: 22.8 us -> 1.9 us
    pallas_call x2, Pallas kernels: 200 us -> 147 us  [attention(): pl.pallas_call(functools.partial(attention_kernel, first, layer, chunks),...]
    pallas_call x1, Pallas kernels: 74 us -> 55.1 us  [head(): pl.pallas_call(functools.partial(head_kernel, chunks, tiles), name='head'...]
    pallas_call x2, Pallas kernels: 193 us -> 205 us  [mlp(): pl.pallas_call(functools.partial(mlp_kernel, first, layer, chunks), name=...]
    another operation x2 -> x0, local copies, waits for them, and re-layouts: 7.89 us -> none  [device_step(): w[l].reshape(dim, width)]
    slice x3 -> x0, local copies, waits for them, and re-layouts: 7.36 us -> none  [device_step(): w[l].reshape(dim, width)]
where the time goes in v3:
time: 414 us; the launch traced here: 413 us
  Pallas kernels  407 us (98%)
    pallas_call x2, Pallas kernels, mlp(): pl.pallas_call(functools.partial(mlp_kernel, first, layer, chunks), name=...  205 us
    pallas_call x2, Pallas kernels, attention(): pl.pallas_call(functools.partial(attention_kernel, first, layer, chunks),...  147 us
    pallas_call x1, Pallas kernels, head(): pl.pallas_call(functools.partial(head_kernel, chunks, tiles), name='head'...  55.1 us

profile of v3, /device:TPU:97, one launch (start us, length us, event | category | flops | bytes accessed | tf_op | source)
XLA Modules:
  0.0 413.5 jit_solution(3899009420938718460)
XLA Ops:
  0.0 0.0 copy-start.1
  0.0 0.0 copy-start
  0.1 2.4 fusion
  2.4 1.5 pad_maximum_fusion
  3.9 0.0 copy-done.1
  3.9 0.0 copy-done
  3.9 0.6 fusion.1
  4.5 72.5 %attention0.1 = (bf16[5,64,2048]{2,1,0:T(8,128)(2,1)}, bf16[4,512,2048]{2,1,0:T(8,128)(2,1)}, bf16[4,1376,256]{2,1,0:T(8,128)(2,1)}, bf16[4,512,256]{2,1,0:T(8,128)(2,1)}, bf16[4,512,256]{2,1,0:T(8,128)(2,1)}) custom-call(bf16[256,2048]{1,0:T(8,128)(2,1)} %refs_1_.3, bf16[1,1024,2048]{2,1,0:T(8,128)(2,1)} %refs_2_.1, f32[1,2048]{1,0:T(1,128)} %get-tuple-element.38.refs_2_, ...), custom_call_target="tpu_custom_call" | custom-call | flops 30000001024 | bytes 30000000 | tf_op jit(solution)/shard_map/attention0/pallas_call | solution.py:427
  77.0 111.9 %mlp0.1 = (bf16[5,64,2048]{2,1,0:T(8,128)(2,1)}, bf16[4,64,2048]{2,1,0:T(8,128)(2,1)}, bf16[5,64,2048]{2,1,0:T(8,128)(2,1)}) custom-call(bf16[5,64,2048]{2,1,0:T(8,128)(2,1)} %get-tuple-element.17.refs_0_, bf16[256,2048]{1,0:T(8,128)(2,1)} %refs_1_.3, bf16[1,1024,2048]{2,1,0:T(8,128)(2,1)} %refs_2_.1, f32[1,2048]{1,0:T(1,128)} %get-tuple-element.30.refs_3_, ...), custom_call_target="tpu_custom_call" | custom-call | flops 80000000000 | bytes 80000000 | tf_op jit(solution)/shard_map/mlp0/pallas_call | solution.py:610
  188.9 74.7 %attention1.1 = (bf16[4,64,2048]{2,1,0:T(8,128)(2,1)}, bf16[4,512,2048]{2,1,0:T(8,128)(2,1)}, bf16[4,1376,256]{2,1,0:T(8,128)(2,1)}) custom-call(bf16[4,64,2048]{2,1,0:T(8,128)(2,1)} %get-tuple-element.20.refs_0_, bf16[5,64,2048]{2,1,0:T(8,128)(2,1)} %get-tuple-element.21.refs_1_, f32[1280,128]{1,0:T(8,128)} %get-tuple-element.36.refs_3_.refs_2_, ...), custom_call_target="tpu_custom_call" | custom-call | flops 30000001024 | bytes 30000000 | tf_op jit(solution)/shard_map/attention1/pallas_call | solution.py:427
  263.6 92.8 %mlp1.1 = (bf16[4,64,2048]{2,1,0:T(8,128)(2,1)}, bf16[4,64,2048]{2,1,0:T(8,128)(2,1)}) custom-call(bf16[4,64,2048]{2,1,0:T(8,128)(2,1)} %get-tuple-element.23.refs_0_, bf16[5,64,2048]{2,1,0:T(8,128)(2,1)} %get-tuple-element.24.refs_1_, f32[1,2048]{1,0:T(1,128)} %get-tuple-element.29.refs_2_, f32[1,2048]{1,0:T(1,128)} %bitcast.11, ...), custom_call_target="tpu_custom_call" | custom-call | flops 80000000000 | bytes 80000000 | tf_op jit(solution)/shard_map/mlp1/pallas_call | solution.py:610
  357.1 55.1 %head.1 = f32[1,1024]{1,0:T(1,128)} custom-call(bf16[4,64,2048]{2,1,0:T(8,128)(2,1)} %get-tuple-element.27.h0, bf16[4,64,2048]{2,1,0:T(8,128)(2,1)} %get-tuple-element.28.h_in, bf16[2048,8192]{1,0:T(8,128)(2,1)} %wv.1, s32[1,1024]{1,0:T(1,128)} %target.1, s32[1]{0:T(128)S(6)} %copy.17.lens), custom_call_target="tpu_custom_call" | custom-call | flops 40000000000 | bytes 40000000 | tf_op jit(solution)/shard_map/head/pallas_call | solution.py:729
  412.2 1.3 copy.18
  (4 shorter events, 0.0 us)
Async XLA Ops:
  0.0 3.9 copy-start.1
  0.0 3.9 copy-start

commit v4 on v3

--- a/solution.py
+++ b/solution.py
@@ -178,11 +178,24 @@
     gather = model_ring(lambda c, b: h_v.at[c, b], h_s, h_r)
     kv = resp_ring(lambda u, b: (k_v, v_v)[u].at[b], kv_s, kv_r)
     ours = ds(r, BLOCK)
-    spread = model_ring(lambda u, b: (wd_y, wo_y, wo_next if first else None)[u].at[b], y_s, y_r, lambda u: (w_down, w_out, w_out)[u].at[layer + u // 2, :, ours])
+    half = w_down.shape[1] // 2
+
+    def spread_piece(u, b):
+        if u < 2:
+            return wd_y.at[b, pl.ds(u * half, half)]
+        return (wo_y, wo_next)[u - 2].at[b]
+
+    def spread_source(u):
+        if u < 2:
+            return w_down.at[layer, pl.ds(u * half, half), ours]
+        return w_out.at[u - 2, :, ours]
+
+    spread = model_ring(spread_piece, y_s, y_r, spread_source)
     shares = spread.places[1:]
     outs = resp_ring(lambda u, b: wo_all.at[shares[u], :, ds(b, BLOCK)], wo_s, wo_r, lambda u: wo_y.at[shares[u]])
 
-    raws = [local(w.at[layer], raw_v.at[i], raw_s.at[i]) for i, w in enumerate(heads_in)]
+    for i, w in enumerate(heads_in):
+        local(w.at[layer], raw_v.at[i], raw_s.at[i])
 
     def x_load(c):
         return pltpu.make_async_copy(xr.at[0, ds(c - 1, BLOCK)], x_v.at[c], load.at[c])
@@ -206,21 +219,23 @@
     def key_block(c):
         return jnp.where(c == 0, r, prompt_blocks + c - 1)
 
-    def flatten():
-        for i, raw in enumerate(raws):
-            raw.wait()
+    def flatten(*which):
+        for i in which:
+            pltpu.make_async_copy(heads_in[i].at[layer], raw_v.at[i], raw_s.at[i]).wait()
 
             def part(n):
                 w_v[i, ds(n, BLOCK)] = raw_v[i, ds(n, BLOCK)].reshape(BLOCK, width)
             loop(0, dim // BLOCK, part)
 
-    def project(c, then=None):
+    def project(c, then=None, queries=True):
         rows = pl.ds(pl.multiple_of(c * BLOCK, BLOCK), BLOCK)
         cs, sn = cos[rows, :], sin[rows, :]
         blk = key_block(c)
         for which in range(3):
             if which == 2 and then is not None:
                 then()
+            if which == 2 and not queries:
+                continue
             for n in range(width // BLOCK):
                 y = dot(h_v[c].reshape(BLOCK, dim), w_v[which, :, pl.ds(n * BLOCK, BLOCK)])
                 for i in range(2):
@@ -246,7 +261,7 @@
     def step(qi, kb, blocks, diagonal=False):
         def scores(n):
             cols = pl.ds(n * LANES, LANES)
-            s = dot_t(k_v[pl.ds(kb, blocks), :, cols].reshape(blocks * BLOCK, LANES), q_v[qi, :, cols])
+            s = dot_t(k_v[pl.ds(kb, blocks), :, cols].reshape(blocks * BLOCK, LANES), q_v[qi, :, cols]) * log_scale
             return jnp.where(causal, s, -jnp.inf) if diagonal else s
 
         kept = [scores(n) for n in range(heads)]
@@ -256,15 +271,13 @@
             if not diagonal:
                 m = m_v[qi, n, :1]
                 top = jnp.maximum(m, top)
-            p = jnp.exp2((s - top) * log_scale)
-            total = jnp.sum(p, axis=0, keepdims=True)
-            p = p.astype(BF)
-            mixed = None
+            total, mixed = 0.0, 0.0
             for b in range(blocks):
-                part = dot(v_v[kb + b, pl.ds(n * LANES, LANES), :], p[b * BLOCK:(b + 1) * BLOCK])
-                mixed = part if mixed is None else mixed + part
+                p = jnp.exp2(s[b * BLOCK:(b + 1) * BLOCK] - top)
+                total = total + jnp.sum(p, axis=0, keepdims=True)
+                mixed = mixed + dot(v_v[kb + b, pl.ds(n * LANES, LANES), :], p.astype(BF))
             if not diagonal:
-                alpha = jnp.exp2((m - top) * log_scale)
+                alpha = jnp.exp2(m - top)
                 total = total + l_v[qi, n, :1] * alpha
                 mixed = mixed + acc_v[qi, n] * alpha
             m_v[qi, n, :1] = top
@@ -291,9 +304,11 @@
     def prompt(qi):
         c = qi - low
         if first:
-            loop(jnp.where(qi == 0, 4 - chip, 1), 4, lambda x: step(qi, 2 * lax.rem(chip + x, 4), 2))
+            side = lax.rem(chip, 2)
+            when((qi > 0) | (side == 1), lambda: step(qi, 2 * (chip + 1 - 2 * side), 2))
+            when((qi > 0) | (chip > 1), lambda: step(qi, 4 * (1 - chip // 2), 4))
         else:
-            loop(jnp.where(qi == 0, 4, 0), 4, lambda x: step(qi, 2 * x, 2))
+            loop(0, jnp.where(qi == 0, 0, 2), lambda x: step(qi, 4 * x, 4))
         for n in range(heads):
             out = (acc_v[qi, n] / l_v[qi, n, :1]).T.astype(BF)
             o_v[c, :, :, pl.ds(n * LANES, LANES)] = out.reshape(4, ROWS, LANES)
@@ -307,14 +322,14 @@
                 getattr(outs, name)(u)
 
     if first:
-        spread.start(1)
-        flatten()
+        spread.start(2)
+        flatten(0, 1)
 
         def chunk(c):
             when(c > 0, lambda: x_load(c).wait())
             norm_rows(lambda cols: x_v[c, :, cols], lambda cols, val: h_v.__setitem__((c, slice(None), slice(None), cols), val.reshape(4, ROWS, BLOCK)), gain, BLOCK, dim)
-            project(c, lambda: when(c == 0, lambda: kv_do('start')))
-            when(c == 1, lambda: (spread.forward(1), spread.start(0)))
+            project(c, lambda: when(c == 0, lambda: (kv_do('start'), flatten(2))))
+            when(c == 1, lambda: (spread.forward(2), spread.start(0), spread.start(1)))
 
         loads[0].wait()
         loop(0, chunks, chunk)
@@ -324,24 +339,25 @@
 
             def pass_on():
                 kv_do('forward')
-                spread.finish(1)
+                spread.finish(2)
                 start_whole_out()
             when(qi == 1, pass_on)
 
         loop(low, chunks, own_and_pass)
+        spread.forward(0)
         for u in range(2):
             kv.mate_has(u, OWN_MATE)
         loop(low, chunks, own_chip)
         kv_do('finish')
-        spread.forward(0)
-        spread.start(2)
+        spread.forward(1)
+        spread.start(3)
         for u in range(2):
             for kind in (LEFT_MATE, RIGHT_MATE, OPP_MATE):
                 kv.mate_has(u, kind)
 
         def prompt_and_events(qi):
             prompt(qi)
-            when(qi == 3, lambda: (whole_out('forward'), spread.forward(2)))
+            when(qi == 3, lambda: (whole_out('forward'), spread.forward(3)))
 
         loop(low, chunks, prompt_and_events)
     else:
@@ -349,19 +365,19 @@
             cp.wait()
         for c in (1, 2):
             gather.start(c)
-        flatten()
-        project(jnp.int32(0))
+        flatten(0, 1)
+        project(jnp.int32(0), queries=False)
         kv_do('start')
+        flatten(2)
 
         def chunk(c):
             def receive():
                 gather.forward(c)
                 when(c + 2 < chunks, lambda: gather.start(c + 2))
             when(c < chunks, receive)
-            when(c == 3, lambda: kv_do('finish', 'mate_arrived'))
-            when(c == 4, lambda: spread.start(0))
-            when(c == 5, lambda: whole_out('forward'))
-            when(c >= 3, lambda: prompt(c - 2))
+            when(c == 4, lambda: (spread.start(0), spread.start(1), kv_do('finish', 'mate_arrived')))
+            when(c == 5, lambda: spread.forward(0))
+            when(c >= 4, lambda: prompt(c - 3))
 
             def use():
                 gather.finish(c - 1)
@@ -369,20 +385,19 @@
                 own(c - 1)
             when((c > 1) & (c <= chunks), use)
             when(c == 2, lambda: (kv_do('forward'), start_whole_out()))
-            when(c == 5, lambda: spread.forward(0))
-
-        loop(1, chunks + 2, chunk)
+            when(c == 5, lambda: (whole_out('forward'), spread.forward(1)))
+
+        loop(1, chunks + 3, chunk)
     whole_out('finish')
-    spread.finish(0)
-    if first:
-        spread.finish(2)
+    for u in (0, 1, 3)[:3 if first else 2]:
+        spread.finish(u)
     for s in range(3):
         outs.mate_arrived(s)
         outs.drain(s)
         own_cols(s).wait()
     for u in range(2):
         kv.drain(u)
-    for u in range(3 if first else 1):
+    for u in range(4 if first else 2):
         spread.drain(u)
     for c in range(chunks - low):
         for k in (1, 2, 3):
@@ -421,7 +436,7 @@
         pltpu.VMEM((outs, 4, ROWS, width), BF),
         sems(chunks),
     ]
-    for kinds, units in ((4, chunks), (8, 2), (4, 3), (8, 3), (3, outs)):
+    for kinds, units in ((4, chunks), (8, 2), (4, 4), (8, 3), (3, outs)):
         scratch += [sems(kinds, units)] * 2
     scratch.append(sems(3))
     return pl.pallas_call(
@@ -468,7 +483,7 @@
         start += [local(rows_in[0].at[pl.ds(1, chunks)], x_v, load.at[1])]
     greet([gather, downs])
     downs.start(2)
-    downs.start(1)
+    downs.start(0)
     for cp in start:
         cp.wait()
 
@@ -507,11 +522,11 @@
             g = dot_t(lhs, wg_v[cols, :])
             inner = (g * jax.nn.sigmoid(g) * dot_t(lhs, wu_v[cols, :])).astype(BF)
             si_v[c, :, :, cols] = inner.reshape(4, ROWS, half)
-        for k in (1, 2, 3):
+        for k in (1, 3, 2):
             i_send(c, k).start()
         ri_v[0, c] = si_v[c, me]
 
-    events = {1: lambda: (downs.forward(2), downs.start(0)), 3: lambda: (downs.forward(1), downs.finish(2))}
+    events = {1: lambda: (downs.forward(2), downs.start(1)), 3: lambda: (downs.forward(0), downs.finish(2))}
 
     def chunk(c):
         def receive():
@@ -527,8 +542,8 @@
             when(c == at, event)
 
     loop(0, chunks + 1, chunk)
-    downs.forward(0)
-    downs.finish(1)
+    downs.forward(1)
+    downs.finish(0)
     for cp in kept:
         cp.wait()
 
@@ -547,7 +562,7 @@
             x_v[lo:hi, :, cols] = acc_v[flat, cols].astype(BF).reshape(shape)
 
         def product(i):
-            q = lax.rem(4 - i, 4)
+            q = jnp.where(i == 1, 3, jnp.maximum(i - 1, 0))
 
             def arrive():
                 for c in range(lo, hi):
@@ -555,7 +570,7 @@
                 if head:
                     downs.mate_arrived(q - 1)
             if head:
-                when(i == 3, lambda: downs.finish(0))
+                when(i == 3, lambda: downs.finish(1))
             else:
                 when(i == 2, lambda: ahead.forward(0))
             when(i > 0, arrive)
@@ -631,7 +646,7 @@
         cols = ds(t, span)
         return pltpu.make_async_copy(wv.at[:, cols], wv_v.at[:, cols], wl.at[t])
 
-    weight(0).start()
+    loop(0, tiles, lambda t: weight(t).start())
     greet([gather])
     for cp in rows:
         cp.wait()
@@ -664,17 +679,12 @@
         l_v[...] = jnp.zeros_like(l_v)
         p_v[...] = jnp.zeros_like(p_v)
         t_v[...] = jnp.broadcast_to(target[:, ds(c, BLOCK)], (LANES, BLOCK)).T - me * vocab
-        when(c == 0, lambda: (weight(0).wait(), weight(1).start()))
+        when(c == 0, lambda: weight(0).wait())
         even_v[...] = logits(c, 0)
 
         def columns(i):
             n = 2 * i
-
-            def next_weight():
-                t = (n + 2) // per
-                weight(t).wait()
-                when(t + 1 < tiles, lambda: weight(t + 1).start())
-            when((c == 0) & (lax.rem(n + 2, per) == 0), next_weight)
+            when((c == 0) & (lax.rem(n + 2, per) == 0), lambda: weight((n + 2) // per).wait())
             when((i == 1) & (c + 1 < chunks), lambda: pass_on(c + 1))
             odd_v[...] = logits(c, n + 1)
             reduce_tile(even_v, n)

time: 414 us -> 406 us (0.981)
  Pallas kernels: 407 us -> 396 us
    pallas_call x2, Pallas kernels: 205 us -> 198 us  [mlp(): pl.pallas_call(functools.partial(mlp_kernel, first, layer, chunks), name=...]
where the time goes in v4:
time: 406 us; the launch traced here: 403 us
  Pallas kernels  396 us (98%)
    pallas_call x2, Pallas kernels, mlp(): pl.pallas_call(functools.partial(mlp_kernel, first, layer, chunks), name=...  198 us
    pallas_call x2, Pallas kernels, attention(): pl.pallas_call(functools.partial(attention_kernel, first, layer, chunks),...  145 us
    pallas_call x1, Pallas kernels, head(): pl.pallas_call(functools.partial(head_kernel, chunks, tiles), name='head'...  52.8 us

profile of v4, /device:TPU:97, one launch (start us, length us, event | category | flops | bytes accessed | tf_op | source)
XLA Modules:
  0.0 402.8 jit_solution(7389310908143312660)
XLA Ops:
  0.0 0.0 copy-start.1
  0.0 0.0 copy-start
  0.1 2.4 fusion
  2.4 1.5 pad_maximum_fusion
  3.9 0.0 copy-done.1
  3.9 0.0 copy-done
  3.9 0.6 fusion.1
  4.5 69.2 %attention0.1 = (bf16[5,64,2048]{2,1,0:T(8,128)(2,1)}, bf16[4,512,2048]{2,1,0:T(8,128)(2,1)}, bf16[4,1376,256]{2,1,0:T(8,128)(2,1)}, bf16[4,512,256]{2,1,0:T(8,128)(2,1)}, bf16[4,512,256]{2,1,0:T(8,128)(2,1)}) custom-call(bf16[256,2048]{1,0:T(8,128)(2,1)} %refs_1_.3, bf16[1,1024,2048]{2,1,0:T(8,128)(2,1)} %refs_2_.1, f32[1,2048]{1,0:T(1,128)} %get-tuple-element.38.refs_2_, ...), custom_call_target="tpu_custom_call" | custom-call | flops 30000001024 | bytes 30000000 | tf_op jit(solution)/shard_map/attention0/pallas_call | solution.py:442
  73.8 107.4 %mlp0.1 = (bf16[5,64,2048]{2,1,0:T(8,128)(2,1)}, bf16[4,64,2048]{2,1,0:T(8,128)(2,1)}, bf16[5,64,2048]{2,1,0:T(8,128)(2,1)}) custom-call(bf16[5,64,2048]{2,1,0:T(8,128)(2,1)} %get-tuple-element.17.refs_0_, bf16[256,2048]{1,0:T(8,128)(2,1)} %refs_1_.3, bf16[1,1024,2048]{2,1,0:T(8,128)(2,1)} %refs_2_.1, f32[1,2048]{1,0:T(1,128)} %get-tuple-element.30.refs_3_, ...), custom_call_target="tpu_custom_call" | custom-call | flops 80000000000 | bytes 80000000 | tf_op jit(solution)/shard_map/mlp0/pallas_call | solution.py:625
  181.2 76.1 %attention1.1 = (bf16[4,64,2048]{2,1,0:T(8,128)(2,1)}, bf16[4,512,2048]{2,1,0:T(8,128)(2,1)}, bf16[4,1376,256]{2,1,0:T(8,128)(2,1)}) custom-call(bf16[4,64,2048]{2,1,0:T(8,128)(2,1)} %get-tuple-element.20.refs_0_, bf16[5,64,2048]{2,1,0:T(8,128)(2,1)} %get-tuple-element.21.refs_1_, f32[1280,128]{1,0:T(8,128)} %get-tuple-element.36.refs_3_.refs_2_, ...), custom_call_target="tpu_custom_call" | custom-call | flops 30000001024 | bytes 30000000 | tf_op jit(solution)/shard_map/attention1/pallas_call | solution.py:442
  257.3 90.8 %mlp1.1 = (bf16[4,64,2048]{2,1,0:T(8,128)(2,1)}, bf16[4,64,2048]{2,1,0:T(8,128)(2,1)}) custom-call(bf16[4,64,2048]{2,1,0:T(8,128)(2,1)} %get-tuple-element.23.refs_0_, bf16[5,64,2048]{2,1,0:T(8,128)(2,1)} %get-tuple-element.24.refs_1_, f32[1,2048]{1,0:T(1,128)} %get-tuple-element.29.refs_2_, f32[1,2048]{1,0:T(1,128)} %bitcast.11, ...), custom_call_target="tpu_custom_call" | custom-call | flops 80000000000 | bytes 80000000 | tf_op jit(solution)/shard_map/mlp1/pallas_call | solution.py:625
  348.7 52.8 %head.1 = f32[1,1024]{1,0:T(1,128)} custom-call(bf16[4,64,2048]{2,1,0:T(8,128)(2,1)} %get-tuple-element.27.h0, bf16[4,64,2048]{2,1,0:T(8,128)(2,1)} %get-tuple-element.28.h_in, bf16[2048,8192]{1,0:T(8,128)(2,1)} %wv.1, s32[1,1024]{1,0:T(1,128)} %target.1, s32[1]{0:T(128)S(6)} %copy.17.lens), custom_call_target="tpu_custom_call" | custom-call | flops 40000000000 | bytes 40000000 | tf_op jit(solution)/shard_map/head/pallas_call | solution.py:739
  401.5 1.3 copy.18
  (4 shorter events, 0.0 us)
Async XLA Ops:
  0.0 3.9 copy-start.1
  0.0 3.9 copy-start
